TPU v7x, 512 devices: a whole 4x4x16 slice. The times are simulated.
512 devices in a mesh: seq: 128 (over x, z, core), head: 4 (over y).
Axes of the slice: x: 4, y: 4, z: 16, core: 2. Of those that a mesh axis runs over, the one named last changes fastest.
Arguments:
- values_in: bfloat16 [65536, 4096], P('seq', 'head'), may hold values from -6 to 6
- gate_in: bfloat16 [65536, 4096], P('seq', 'head'), may hold values from -6 to 6
- key_proj: bfloat16 [65536, 128], P('seq'), may hold values from -0.52734375 to 0.52734375
- query_proj: bfloat16 [65536, 128], P('seq'), may hold values from -6 to 6
- step_size: float32 [65536, 64], P('seq', 'head'), may hold values from 0.5 to 2
- log_decay: float32 [65536, 64], P('seq', 'head'), may hold values from -1.2 to 0
- skip_weight: float32 [64], P('head'), may hold values from 0.5 to 1.5
- norm_gain: float32 [4096], P('head'), may hold values from 0.5 to 1.5
- level_table: float32 [16, 64, 11], P(None, 'head'), may hold values from 0.25 to 2
- level_pick: int32 [65536], P('seq'), may hold values from 0 to 15
- doc_start: int32 [1024], P('seq'), may hold values 0 or 1
Outputs:
- layer_out: bfloat16 [65536, 4096], P('seq', 'head')
All inputs are finite; a program needn't handle non-finite values. No bound on the sum of `doc_start` on one device may be relied on, other than what follows from the above.
Results may differ from a plain program's by a relative error of at most 0.012.
Values may be sent and summed in bfloat16 or wider, within the bound.
A program may use at most 64 MiB of HBM per device.

v0:
```python
import math

import jax
import jax.numpy as jnp
from jax import lax
from jax.sharding import Mesh
from jax.sharding import PartitionSpec as P

H = 64
HEADDIM = 64
STRETCH = 64
SEQ = ("seq_0", "seq_1", "seq_2")


epsilon = 1e-06


def joined_along(pieces, dim):
    pieces = jnp.moveaxis(pieces, 0, dim)
    shape = pieces.shape
    return pieces.reshape(*shape[:dim], shape[dim] * shape[dim + 1], *shape[dim + 2 :])


def gather_in_order(array, axes, turns):
    pieces = array[None]
    for k in turns:
        pieces = lax.all_gather(pieces, axes[k], axis=0, tiled=True)
    current = [lax.axis_size(axes[k]) for k in reversed(turns)]
    pieces = pieces.reshape(*current, *array.shape)
    turned = sorted(range(len(turns)), key=lambda place: turns[len(turns) - 1 - place])
    return pieces.transpose(*turned, *range(len(turns), pieces.ndim)).reshape(-1, *array.shape)


def gathered_by_axis(array, axes, turns, dim):
    return joined_along(gather_in_order(array, axes, turns), dim)


def copy_for_each(array, axis):
    size = lax.axis_size(axis)
    return lax.all_to_all(
        jnp.broadcast_to(array[None], (size, *array.shape)), axis, 0, 0, tiled=True
    )


def over_copies(array, axis):
    everything = copy_for_each(array, axis)
    return jnp.sum(everything, axis=0)


def level_of_pairs(row_count, stretch_len, low_bits):
    blocks = jnp.arange(row_count, dtype=jnp.int32) // stretch_len
    differ = jnp.bitwise_xor(blocks[:, None], blocks[None, :])
    level_index = jnp.zeros((row_count, row_count), jnp.int32)
    for bit_index in range(low_bits):
        level_index = level_index + (differ >= 1 << bit_index).astype(jnp.int32)
    return level_index


def flip_pairs(tensor, bit_index):
    split_view = tensor.reshape(
        (tensor.shape[0] >> bit_index + 1, 2, 1 << bit_index) + tensor.shape[1:]
    )
    return split_view[:, ::-1].reshape(tensor.shape)


def local(
    values_in,
    gate_in,
    key_proj,
    query_proj,
    step_size,
    log_decay,
    skip_weight,
    norm_gain,
    level_table,
    level_pick,
    doc_start,
):
    tok_rows = values_in.shape[0]
    head_count = step_size.shape[1]
    head_width = HEADDIM
    state_width = key_proj.shape[1]
    per_span = doc_start.shape[0]
    low_bits = per_span.bit_length() - 1
    span_total = lax.axis_size(SEQ)
    span_bits = span_total.bit_length() - 1
    table_rows = level_table.shape[0]
    level_count = level_table.shape[2]
    one_hot = (level_pick[:, None] == jnp.arange(table_rows, dtype=jnp.int32)[None, :]).astype(
        jnp.float32
    )
    level_weight = jnp.dot(
        one_hot,
        level_table.reshape(table_rows, head_count * level_count),
        precision=lax.Precision.HIGHEST,
        preferred_element_type=jnp.float32,
    ).reshape(tok_rows, head_count, level_count)
    log_total = jnp.cumsum(log_decay, axis=0)
    doc_stretch = jnp.cumsum(doc_start)
    doc_count = jnp.broadcast_to(doc_stretch[:, None], (per_span, STRETCH)).reshape(tok_rows)
    scaled_in = (jnp.repeat(step_size, head_width, axis=1) * values_in.astype(jnp.float32)).astype(
        jnp.bfloat16
    )
    end_log = log_total[tok_rows - 1]
    tail_decay = (
        jnp.exp(end_log[None, :] - log_total)
        * (doc_count == doc_count[tok_rows - 1]).astype(jnp.float32)[:, None]
    )
    carried_in = (
        jnp.repeat(tail_decay, head_width, axis=1) * scaled_in.astype(jnp.float32)
    ).astype(jnp.bfloat16)
    end_state = jnp.einsum("sc,sn->cn", carried_in, key_proj, preferred_element_type=jnp.float32)
    span_decay = jnp.exp(end_log) * (doc_count[tok_rows - 1] == 0).astype(jnp.float32)
    own_index = lax.axis_index(SEQ)
    row_share = head_count * head_width // span_total
    pieces = lax.all_to_all(
        end_state.reshape(1, head_count * head_width, state_width).astype(jnp.bfloat16),
        SEQ,
        split_axis=1,
        concat_axis=0,
        tiled=True,
    ).astype(jnp.float32)
    decays = gathered_by_axis(span_decay.reshape(1, head_count), SEQ, (0, 1, 2), 0)
    row_head = (own_index * row_share + jnp.arange(row_share, dtype=jnp.int32)) // head_width
    head_pick = (row_head[:, None] == jnp.arange(head_count, dtype=jnp.int32)[None, :]).astype(
        jnp.float32
    )
    block_decay = jnp.dot(
        decays, head_pick.T, precision=lax.Precision.HIGHEST, preferred_element_type=jnp.float32
    )
    block_state = pieces
    lead_decay = jnp.ones_like(block_decay)
    span_range = jnp.arange(span_total, dtype=jnp.int32)
    level_list = []
    for bit_index in range(span_bits):
        other_state = flip_pairs(block_state, bit_index)
        other_decay = flip_pairs(block_decay, bit_index)
        is_upper = span_range >> bit_index & 1 == 1
        level_list.append(
            jnp.where(is_upper[:, None, None], lead_decay[:, :, None] * other_state, 0.0)
        )
        block_state = jnp.where(
            is_upper[:, None, None],
            block_state + block_decay[:, :, None] * other_state,
            other_state + other_decay[:, :, None] * block_state,
        )
        lead_decay = jnp.where(is_upper[:, None], lead_decay * other_decay, lead_decay)
        block_decay = block_decay * other_decay
    level_all = jnp.stack(level_list, 1).astype(jnp.bfloat16)
    returned = lax.all_to_all(level_all, SEQ, split_axis=0, concat_axis=2, tiled=True)
    remote_state = returned.reshape(span_bits, head_count, head_width, state_width)
    level_index = level_of_pairs(tok_rows, STRETCH, low_bits)
    element_position = jnp.arange(tok_rows, dtype=jnp.int32)
    visible = (element_position[:, None] >= element_position[None, :]) & (
        doc_count[:, None] == doc_count[None, :]
    )
    scores = jnp.einsum("tn,sn->ts", query_proj, key_proj, preferred_element_type=jnp.float32)
    reach_decay = jnp.exp(log_total) * (doc_count == 0).astype(jnp.float32)[:, None]
    group_size = math.gcd(head_count, 4)
    group_count = head_count // group_size

    def head_group(inputs):
        group_log, group_weight, group_scaled, group_remote, group_reach = inputs
        select = jnp.zeros((group_size, tok_rows, tok_rows), jnp.float32)
        for level_id in range(low_bits + 1):
            select = select + jnp.where(
                level_index[None] == level_id,
                jnp.transpose(group_weight[:, :, level_id])[:, :, None],
                0.0,
            )
        log_rows = jnp.transpose(group_log)
        log_gap = jnp.where(visible[None], log_rows[:, :, None] - log_rows[:, None, :], -jnp.inf)
        mixing = (scores[None] * select * jnp.exp(log_gap)).astype(jnp.bfloat16)
        local_part = jnp.einsum(
            "hts,shp->thp",
            mixing,
            group_scaled.reshape(tok_rows, group_size, head_width),
            preferred_element_type=jnp.float32,
        )
        projected = jnp.einsum(
            "tn,bhpn->tbhp", query_proj, group_remote, preferred_element_type=jnp.float32
        )
        remote_weight = group_weight[:, :, 1 + low_bits : 1 + low_bits + span_bits]
        remote_part = group_reach[:, :, None] * jnp.einsum(
            "thb,tbhp->thp", remote_weight, projected, precision=lax.Precision.HIGHEST
        )
        return (local_part + remote_part).reshape(tok_rows, group_size * head_width)

    stacked = (
        log_total.reshape(tok_rows, group_count, group_size).transpose(1, 0, 2),
        level_weight.reshape(tok_rows, group_count, group_size, level_count).transpose(1, 0, 2, 3),
        scaled_in.reshape(tok_rows, group_count, group_size * head_width).transpose(1, 0, 2),
        remote_state.reshape(span_bits, group_count, group_size, head_width, state_width).transpose(
            1, 0, 2, 3, 4
        ),
        reach_decay.reshape(tok_rows, group_count, group_size).transpose(1, 0, 2),
    )
    group_parts = lax.map(head_group, stacked)
    both_parts = group_parts.transpose(1, 0, 2).reshape(tok_rows, head_count * head_width)
    combined = both_parts + jnp.repeat(skip_weight, head_width)[None, :] * values_in.astype(
        jnp.float32
    )
    gated_out = combined * jax.nn.silu(gate_in.astype(jnp.float32))
    square_sum = over_copies(jnp.sum(gated_out * gated_out, axis=1), "head")
    mean_square = square_sum / (H * HEADDIM)
    return (gated_out * lax.rsqrt(mean_square + epsilon)[:, None] * norm_gain[None, :]).astype(
        jnp.bfloat16
    )


def solution(mesh):
    split = Mesh(
        mesh.devices.reshape(4, 16, 2, mesh.shape["head"]), ("seq_0", "seq_1", "seq_2", "head")
    )
    placed = (
        P(SEQ, "head"),
        P(SEQ, "head"),
        P(SEQ, None),
        P(SEQ, None),
        P(SEQ, "head"),
        P(SEQ, "head"),
        P("head"),
        P("head"),
        P(None, "head", None),
        P(SEQ),
        P(SEQ),
    )
    return jax.shard_map(
        local, mesh=split, in_specs=placed, out_specs=P(SEQ, "head"), check_vma=False
    )
```

profile of v0, /device:TPU:6, one launch (start us, length us, event | category | flops | bytes accessed | tf_op | source)
XLA Modules:
  0.0 270.3 jit_solution(7450920758946439737)
XLA Ops:
  0.0 0.9 reduce-window.18
  2.9 0.8 copy_bitcast_fusion
  3.7 1.1 reduce-window.19
  5.1 1.5 copy.349
  6.8 0.8 exponential_multiply_fusion.1
  7.6 1.4 fusion.30
  10.4 2.2 reduce.9
  12.6 0.8 reshape.1288
  13.4 19.9 %all-to-all-start = ((bf16[128,2,512]{2,1,0:T(2,128)(2,1)}), bf16[128,2,512]{2,1,0:T(2,128)(2,1)S(1)}, u32[]{:S(2)}, u32[]{:S(2)}) async-start(bf16[128,2,512]{2,1,0:T(2,128)(2,1)} %reshape.1288), calls=%async_computation | async-start | bytes 524288 | tf_op jit(solution)/shard_map/all_to_all | solution.py:116
  33.5 6.7 %all-gather.3 = f32[4,1,16]{2,1,0:T(1,128)S(1)} all-gather(f32[1,1,16]{2,1,0:T(1,128)S(1)} %bitcast.339), channel_id=2, replica_groups=mesh['seq_0'=4,'seq_1'=16,'seq_2'=2,'head'=4] {'seq_0'}, dimensions={0}, use_global_device_ids=true | all-gather | bytes 320 | tf_op jit(solution)/shard_map/all_gather | solution.py:27
  40.2 29.8 %all-gather.4 = f32[16,4,16]{2,1,0:T(4,128)S(1)} all-gather(f32[1,4,16]{2,1,0:T(4,128)S(1)} %bitcast.338), channel_id=3, replica_groups=mesh['seq_0'=4,'seq_1'=16,'seq_2'=2,'head'=4] {'seq_1'}, dimensions={0}, use_global_device_ids=true | all-gather | bytes 4352 | tf_op jit(solution)/shard_map/all_gather | solution.py:27
  70.1 2.0 all-gather.5
  75.2 0.7 copy.435
  76.6 0.7 copy.444
  77.7 0.7 copy.360
  78.5 0.7 copy.366
  79.2 0.7 copy.376
  80.6 0.7 copy.390
  81.4 0.7 copy.398
  86.9 1.0 add_select_fusion.4
  87.9 2.5 add_select_fusion.3
  90.4 1.1 rev.45
  91.5 2.8 %add_select_fusion.2 = f32[4,2,16,8,128]{4,3,2,1,0:T(8,128)} fusion(f32[4,2,16,8,128]{4,3,2,1,0:T(8,128)S(1)} %bitcast.269, f32[4,2,16,8,128]{4,3,2,1,0:T(8,128)S(1)} %bitcast.265, f32[4,2,16,8,128]{4,3,2,1,0:T(8,128)S(1)} %bitcast.260, f32[4,2,16,8,128]{4,3,2,1,0:T(8,128)S(1)} %bitcast.247, f32[4,2,16,8,128]{4,3,2,1,0:T(8,128)S(1)} %bitcast.255, ...), kind=kLoop, calls=%fused_computation.60 | loop fusion | flops 2621440 | bytes 3179008 | tf_op jit(solution)/shard_map/jit(_where)/select_n | solution.py:142
  94.3 1.1 rev.47
  95.4 5.8 %add_select_fusion.1 = f32[2,2,32,8,128]{4,3,2,1,0:T(8,128)} fusion(f32[2,2,32,8,128]{4,3,2,1,0:T(8,128)S(1)} %bitcast.274, f32[2,2,32,8,128]{4,3,2,1,0:T(8,128)S(1)} %bitcast.270, f32[2,2,32,8,128]{4,3,2,1,0:T(8,128)S(1)} %bitcast.266, f32[2,2,32,8,128]{4,3,2,1,0:T(8,128)S(1)} %bitcast.261, f32[2,2,32,8,128]{4,3,2,1,0:T(8,128)S(1)} %bitcast.248, ...), kind=kLoop, calls=%fused_computation.58 | loop fusion | flops 3276800 | bytes 3711616 | tf_op jit(solution)/shard_map/jit(_where)/select_n | solution.py:142
  101.2 1.9 rev.49
  103.1 6.6 %add_select_fusion = f32[1,2,64,8,128]{4,3,2,1,0:T(8,128)} fusion(f32[1,2,64,8,128]{4,3,2,1,0:T(8,128)} %bitcast.279, f32[1,2,64,8,128]{4,3,2,1,0:T(8,128)S(1)} %bitcast.275, f32[1,2,64,8,128]{4,3,2,1,0:T(8,128)S(1)} %bitcast.271, f32[1,2,64,8,128]{4,3,2,1,0:T(8,128)S(1)} %bitcast.267, f32[1,2,64,8,128]{4,3,2,1,0:T(8,128)S(1)} %bitcast.262, ...), kind=kLoop, calls=%fused_computation.56 | loop fusion | flops 3932160 | bytes 4244224 | tf_op jit(solution)/shard_map/jit(_where)/select_n | solution.py:142
  109.8 1.9 rev.51
  111.7 0.9 fusion.32
  112.6 2.0 fusion.33
  114.6 1.1 fusion.34
  115.7 1.1 fusion.35
  116.8 1.1 fusion.36
  117.9 1.1 fusion.37
  119.0 1.1 fusion.38
  120.0 15.1 %all-to-all-start.1 = ((bf16[128,7,8,128]{3,2,1,0:T(8,128)(2,1)}), bf16[128,7,8,128]{3,2,1,0:T(8,128)(2,1)S(1)}, u32[]{:S(2)}, u32[]{:S(2)}) async-start(bf16[128,7,8,128]{3,2,1,0:T(8,128)(2,1)} %fusion.38), calls=%async_computation.1 | async-start | bytes 3670016 | tf_op jit(solution)/shard_map/all_to_all | solution.py:150
  136.4 1.3 copy.411
  137.9 1.2 fusion.50
  139.1 82.7 %all-to-all-done.1 = bf16[128,7,8,128]{3,2,1,0:T(8,128)(2,1)S(1)} async-done(((bf16[128,7,8,128]{3,2,1,0:T(8,128)(2,1)}), bf16[128,7,8,128]{3,2,1,0:T(8,128)(2,1)S(1)}, u32[]{:S(2)}, u32[]{:S(2)}) %all-to-all-start.1) | async-done | bytes 1835040 | tf_op jit(solution)/shard_map/all_to_all | solution.py:150
  221.8 1.6 copy.408
  223.3 32.9 %while.12 = (s32[]{:T(128)}, f32[4,512,256]{1,2,0:T(8,128)}, bf16[4,512,256]{1,2,0:T(8,128)(2,1)}, f32[512,512]{1,0:T(8,128)S(1)}, f32[4,512,4,11]{1,2,3,0:T(4,1...) while((s32[]{:T(128)}, f32[4,512,256]{1,2,0:T(8,128)}, ...), condition=%wide.region_4.5_spmd.clone.clone, body=%wide.region_3.4_spmd.clone.clone.sunk | while | flops 387842048 | bytes 8172673 | solution.py:198
  223.4 1.8 fusion.70
  225.2 1.0 constant_dynamic-slice_fusion.2
  226.2 0.9 fusion.69
  227.4 3.4 %fusion.71 = f32[512,4,64]{0,2,1:T(8,128)S(1)} fusion(bf16[512,4,64]{0,2,1:T(8,128)(2,1)S(1)} %bitcast.277, f32[4,512]{1,0:T(4,128)S(1)} %get-tuple-element.349, f32[4,512]{1,0:T(4,128)S(1)} %get-tuple-element.350, f32[4,512]{1,0:T(4,128)S(1)} %get-tuple-element.351, f32[4,512]{1,0:T(4,128)S(1)} %get-tuple-element.352, ...), kind=kOutput, calls=%fused_computation.15.clone.1 | convolution fusion | flops 147062784 | bytes 3719168 | tf_op jit(solution)/shard_map/while/body/eval_jaxpr/hts,shp->thp/dot_general | solution.py:174
  230.8 0.9 constant_dynamic-update-slice_fusion.2
  231.7 1.7 fusion.70
  233.4 1.0 constant_dynamic-slice_fusion.2
  234.4 0.9 fusion.69
  235.6 3.4 %fusion.71 = f32[512,4,64]{0,2,1:T(8,128)S(1)} fusion(bf16[512,4,64]{0,2,1:T(8,128)(2,1)S(1)} %bitcast.277, f32[4,512]{1,0:T(4,128)S(1)} %get-tuple-element.349, f32[4,512]{1,0:T(4,128)S(1)} %get-tuple-element.350, f32[4,512]{1,0:T(4,128)S(1)} %get-tuple-element.351, f32[4,512]{1,0:T(4,128)S(1)} %get-tuple-element.352, ...), kind=kOutput, calls=%fused_computation.15.clone.1 | convolution fusion | flops 147062784 | bytes 3719168 | tf_op jit(solution)/shard_map/while/body/eval_jaxpr/hts,shp->thp/dot_general | solution.py:174
  239.0 0.8 constant_dynamic-update-slice_fusion.2
  239.9 1.7 fusion.70
  241.6 1.0 constant_dynamic-slice_fusion.2
  242.6 0.9 fusion.69
  243.8 3.4 %fusion.71 = f32[512,4,64]{0,2,1:T(8,128)S(1)} fusion(bf16[512,4,64]{0,2,1:T(8,128)(2,1)S(1)} %bitcast.277, f32[4,512]{1,0:T(4,128)S(1)} %get-tuple-element.349, f32[4,512]{1,0:T(4,128)S(1)} %get-tuple-element.350, f32[4,512]{1,0:T(4,128)S(1)} %get-tuple-element.351, f32[4,512]{1,0:T(4,128)S(1)} %get-tuple-element.352, ...), kind=kOutput, calls=%fused_computation.15.clone.1 | convolution fusion | flops 147062784 | bytes 3719168 | tf_op jit(solution)/shard_map/while/body/eval_jaxpr/hts,shp->thp/dot_general | solution.py:174
  247.2 0.9 constant_dynamic-update-slice_fusion.2
  248.1 1.7 fusion.70
  249.9 1.0 constant_dynamic-slice_fusion.2
  250.8 0.9 fusion.69
  252.0 3.4 %fusion.71 = f32[512,4,64]{0,2,1:T(8,128)S(1)} fusion(bf16[512,4,64]{0,2,1:T(8,128)(2,1)S(1)} %bitcast.277, f32[4,512]{1,0:T(4,128)S(1)} %get-tuple-element.349, f32[4,512]{1,0:T(4,128)S(1)} %get-tuple-element.350, f32[4,512]{1,0:T(4,128)S(1)} %get-tuple-element.351, f32[4,512]{1,0:T(4,128)S(1)} %get-tuple-element.352, ...), kind=kOutput, calls=%fused_computation.15.clone.1 | convolution fusion | flops 147062784 | bytes 3719168 | tf_op jit(solution)/shard_map/while/body/eval_jaxpr/hts,shp->thp/dot_general | solution.py:174
  255.4 0.8 constant_dynamic-update-slice_fusion.2
  256.3 2.8 %multiply_reduce_fusion = (f32[512]{0:T(512)S(1)}, f32[512,1024]{0,1:T(8,128)S(1)}) fusion(bf16[512,1024]{0,1:T(8,128)(2,1)} %copy.411, bf16[512,1024]{0,1:T(8,128)(2,1)S(1)} %copy-done.2, f32[1024]{0:T(1024)S(1)} %mul.848, f32[4,512,256]{1,2,0:T(8,128)} %get-tuple-element.71), kind=kLoop, calls=%fused_computation.51 | loop fusion | flops 5766656 | bytes 6297600 | tf_op jit(solution)/shard_map/reduce_sum | solution.py:204
  259.1 9.6 %all_to_all.30 = f32[4,1,512]{2,1,0:T(1,128)S(1)} all-to-all(f32[4,1,512]{2,1,0:T(1,128)S(1)} %broadcast_in_dim.337), channel_id=1, replica_groups=mesh['seq_0'=4,'seq_1'=16,'seq_2'=2,'head'=4] {'head'}, dimensions={0} | all-to-all | bytes 16384 | tf_op jit(solution)/shard_map/all_to_all | solution.py:40
  269.0 1.3 copy.413
  (184 shorter events, 15.6 us)
Async XLA Ops:
  0.0 9.0 %copy-start = (bf16[512,128]{1,0:T(8,128)(2,1)S(1)}, bf16[512,128]{1,0:T(8,128)(2,1)}, u32[]{:S(2)}) copy-start(bf16[512,128]{1,0:T(8,128)(2,1)} %param.15) | copy-start | bytes 393220
  0.0 7.6 %copy-start.19 = (f32[512,16]{0,1:T(8,128)S(1)}, f32[512,16]{0,1:T(8,128)}, u32[]{:S(2)}) copy-start(f32[512,16]{0,1:T(8,128)} %param.17) | copy-start | bytes 98308
  5.1 3.9 %copy-start.15 = (f32[512,16]{0,1:T(8,128)}, f32[512,16]{0,1:T(8,128)S(1)}, u32[]{:S(2)}) copy-start(f32[512,16]{0,1:T(8,128)S(1)} %bitcast_bitcast_fusion) | copy-start | bytes 98308
  6.6 2.8 %copy-start.1 = (bf16[512,1024]{0,1:T(8,128)(2,1)}, bf16[512,1024]{0,1:T(8,128)(2,1)S(1)}, u32[]{:S(2)}) copy-start(bf16[512,1024]{0,1:T(8,128)(2,1)S(1)} %copy.349) | copy-start | bytes 3145732
  13.4 72.1 %all-to-all-start = ((bf16[128,2,512]{2,1,0:T(2,128)(2,1)}), bf16[128,2,512]{2,1,0:T(2,128)(2,1)S(1)}, u32[]{:S(2)}, u32[]{:S(2)}) async-start(bf16[128,2,512]{2,1,0:T(2,128)(2,1)} %reshape.1288), calls=%async_computation | async-start | bytes 524288 | tf_op jit(solution)/shard_map/all_to_all | solution.py:116
  33.4 40.8 %copy-start.22 = (pred[128]{0:T(512)(128)(4,1)}, pred[128]{0:T(512)(128)(4,1)S(1)}, u32[]{:S(2)}) copy-start(pred[128]{0:T(512)(128)(4,1)S(1)} %get-tuple-element.252) | copy-start | bytes 388
  33.4 40.8 %copy-start.24 = (pred[128]{0:T(512)(128)(4,1)}, pred[128]{0:T(512)(128)(4,1)S(1)}, u32[]{:S(2)}) copy-start(pred[128]{0:T(512)(128)(4,1)S(1)} %get-tuple-element.253) | copy-start | bytes 388
  33.4 40.8 %copy-start.26 = (pred[128]{0:T(512)(128)(4,1)}, pred[128]{0:T(512)(128)(4,1)S(1)}, u32[]{:S(2)}) copy-start(pred[128]{0:T(512)(128)(4,1)S(1)} %get-tuple-element.254) | copy-start | bytes 388
  33.4 40.8 %copy-start.28 = (pred[128]{0:T(512)(128)(4,1)}, pred[128]{0:T(512)(128)(4,1)S(1)}, u32[]{:S(2)}) copy-start(pred[128]{0:T(512)(128)(4,1)S(1)} %get-tuple-element.255) | copy-start | bytes 388
  33.5 40.8 %copy-start.30 = (pred[128]{0:T(512)(128)(4,1)}, pred[128]{0:T(512)(128)(4,1)S(1)}, u32[]{:S(2)}) copy-start(pred[128]{0:T(512)(128)(4,1)S(1)} %get-tuple-element.256) | copy-start | bytes 388
  33.5 40.8 %copy-start.32 = (pred[128]{0:T(512)(128)(4,1)}, pred[128]{0:T(512)(128)(4,1)S(1)}, u32[]{:S(2)}) copy-start(pred[128]{0:T(512)(128)(4,1)S(1)} %get-tuple-element.257) | copy-start | bytes 388
  73.1 18.4 %copy-start.4 = (f32[128,8]{1,0:T(8,128)}, f32[128,8]{1,0:T(8,128)S(1)}, u32[]{:S(2)}) copy-start(f32[128,8]{1,0:T(8,128)S(1)} %copy.374) | copy-start | bytes 12292
  73.1 18.4 %copy-start.5 = (f32[16,2,4,8]{3,2,1,0:T(4,128)}, f32[16,2,4,8]{3,2,1,0:T(4,128)S(1)}, u32[]{:S(2)}) copy-start(f32[16,2,4,8]{3,2,1,0:T(4,128)S(1)} %rev.44) | copy-start | bytes 12292
  74.4 17.1 %copy-start.7 = (f32[8,2,8,8]{3,2,1,0:T(8,128)}, f32[8,2,8,8]{3,2,1,0:T(8,128)S(1)}, u32[]{:S(2)}) copy-start(f32[8,2,8,8]{3,2,1,0:T(8,128)S(1)} %copy.429) | copy-start | bytes 12292
  74.5 17.1 %copy-start.8 = (f32[128,8]{1,0:T(8,128)}, f32[128,8]{1,0:T(8,128)S(1)}, u32[]{:S(2)}) copy-start(f32[128,8]{1,0:T(8,128)S(1)} %copy.428) | copy-start | bytes 12292
  103.1 8.6 %copy-start.33 = (pred[128]{0:T(512)(128)(4,1)S(1)}, pred[128]{0:T(512)(128)(4,1)}, u32[]{:S(2)}) copy-start(pred[128]{0:T(512)(128)(4,1)} %copy-done.32) | copy-start | bytes 388
  103.1 9.5 %copy-start.31 = (pred[128]{0:T(512)(128)(4,1)S(1)}, pred[128]{0:T(512)(128)(4,1)}, u32[]{:S(2)}) copy-start(pred[128]{0:T(512)(128)(4,1)} %copy-done.30) | copy-start | bytes 388
  109.7 4.9 %copy-start.14 = (f32[128,8]{1,0:T(8,128)S(1)}, f32[128,8]{1,0:T(8,128)}, u32[]{:S(2)}) copy-start(f32[128,8]{1,0:T(8,128)} %copy.366) | copy-start | bytes 12292
  109.7 4.9 %copy-start.29 = (pred[128]{0:T(512)(128)(4,1)S(1)}, pred[128]{0:T(512)(128)(4,1)}, u32[]{:S(2)}) copy-start(pred[128]{0:T(512)(128)(4,1)} %copy-done.28) | copy-start | bytes 388
  109.7 6.0 %copy-start.13 = (f32[128,8]{1,0:T(8,128)S(1)}, f32[128,8]{1,0:T(8,128)}, u32[]{:S(2)}) copy-start(f32[128,8]{1,0:T(8,128)} %copy.376) | copy-start | bytes 12292
  109.7 6.0 %copy-start.27 = (pred[128]{0:T(512)(128)(4,1)S(1)}, pred[128]{0:T(512)(128)(4,1)}, u32[]{:S(2)}) copy-start(pred[128]{0:T(512)(128)(4,1)} %copy-done.26) | copy-start | bytes 388
  109.7 7.1 %copy-start.12 = (f32[128,8]{1,0:T(8,128)S(1)}, f32[128,8]{1,0:T(8,128)}, u32[]{:S(2)}) copy-start(f32[128,8]{1,0:T(8,128)} %copy.384) | copy-start | bytes 12292
  109.7 7.1 %copy-start.25 = (pred[128]{0:T(512)(128)(4,1)S(1)}, pred[128]{0:T(512)(128)(4,1)}, u32[]{:S(2)}) copy-start(pred[128]{0:T(512)(128)(4,1)} %copy-done.24) | copy-start | bytes 388
  111.7 6.2 %copy-start.3 = (f32[2,2,32,8,128]{4,3,2,1,0:T(8,128)S(1)}, f32[2,2,32,8,128]{4,3,2,1,0:T(8,128)}, u32[]{:S(2)}) copy-start(f32[2,2,32,8,128]{4,3,2,1,0:T(8,128)} %rev.49) | copy-start | bytes 1572868
  111.7 6.2 %copy-start.11 = (f32[128,8]{1,0:T(8,128)S(1)}, f32[128,8]{1,0:T(8,128)}, u32[]{:S(2)}) copy-start(f32[128,8]{1,0:T(8,128)} %copy.390) | copy-start | bytes 12292
  111.7 6.2 %copy-start.23 = (pred[128]{0:T(512)(128)(4,1)S(1)}, pred[128]{0:T(512)(128)(4,1)}, u32[]{:S(2)}) copy-start(pred[128]{0:T(512)(128)(4,1)} %copy-done.22) | copy-start | bytes 388
  112.6 6.3 %copy-start.6 = (f32[1,2,64,8,128]{4,3,2,1,0:T(8,128)S(1)}, f32[1,2,64,8,128]{4,3,2,1,0:T(8,128)}, u32[]{:S(2)}) copy-start(f32[1,2,64,8,128]{4,3,2,1,0:T(8,128)} %rev.51) | copy-start | bytes 1572868
  112.6 6.3 %copy-start.10 = (f32[128,8]{1,0:T(8,128)S(1)}, f32[128,8]{1,0:T(8,128)}, u32[]{:S(2)}) copy-start(f32[128,8]{1,0:T(8,128)} %copy.398) | copy-start | bytes 12292
  112.6 6.3 %copy-start.34 = (pred[128]{0:T(512)(128)(4,1)S(1)}, pred[128]{0:T(512)(128)(4,1)}, u32[]{:S(2)}) copy-start(pred[128]{0:T(512)(128)(4,1)} %and_compare_fusion.21) | copy-start | bytes 388
  119.0 16.2 %copy-start.16 = (f32[512,16]{0,1:T(8,128)S(1)}, f32[512,16]{0,1:T(8,128)}, u32[]{:S(2)}) copy-start(f32[512,16]{0,1:T(8,128)} %copy-done.15) | copy-start | bytes 98308
  119.0 16.2 %copy-start.17 = (f32[512,16]{0,1:T(8,128)S(1)}, f32[512,16]{0,1:T(8,128)}, u32[]{:S(2)}) copy-start(f32[512,16]{0,1:T(8,128)} %get-tuple-element.248) | copy-start | bytes 98308
  120.0 15.2 %copy-start.18 = (f32[16,16,11]{1,0,2:T(8,128)S(1)}, f32[16,16,11]{1,0,2:T(8,128)}, u32[]{:S(2)}) copy-start(f32[16,16,11]{1,0,2:T(8,128)} %param.21) | copy-start | bytes 33796
  120.0 15.7 %copy-start.21 = (s32[512]{0:T(512)S(1)}, s32[512]{0:T(512)}, u32[]{:S(2)}) copy-start(s32[512]{0:T(512)} %param.22) | copy-start | bytes 6148
  120.0 16.3 %copy-start.9 = (bf16[512,1024]{1,0:T(8,128)(2,1)S(1)}, bf16[512,1024]{1,0:T(8,128)(2,1)}, u32[]{:S(2)}) copy-start(bf16[512,1024]{1,0:T(8,128)(2,1)} %param.14) | copy-start | bytes 3145732
  120.0 101.7 %all-to-all-start.1 = ((bf16[128,7,8,128]{3,2,1,0:T(8,128)(2,1)}), bf16[128,7,8,128]{3,2,1,0:T(8,128)(2,1)S(1)}, u32[]{:S(2)}, u32[]{:S(2)}) async-start(bf16[128,7,8,128]{3,2,1,0:T(8,128)(2,1)} %fusion.38), calls=%async_computation.1 | async-start | bytes 3670016 | tf_op jit(solution)/shard_map/all_to_all | solution.py:150
  135.2 2.5 copy-start.35
  223.3 32.9 %copy-start.2 = (bf16[512,1024]{0,1:T(8,128)(2,1)S(1)}, bf16[512,1024]{0,1:T(8,128)(2,1)}, u32[]{:S(2)}) copy-start(bf16[512,1024]{0,1:T(8,128)(2,1)} %copy-done.1) | copy-start | bytes 3145732
  256.3 12.4 %copy-start.20 = (f32[1024]{0:T(1024)S(1)}, f32[1024]{0:T(1024)}, u32[]{:S(2)}) copy-start(f32[1024]{0:T(1024)} %param.20) | copy-start | bytes 12292
where the time goes:
time: 273 us; the launch traced here: 270 us
  waiting for transfers between devices  82.7 us (30%)
  blocking collectives  48.1 us (18%)
  other arithmetic  46.5 us (17%)
  starting transfers between devices  35 us (13%)
  local copies, waits for them, and re-layouts  33.5 us (12%)
  matrix products  22.9 us (8%)
    all_to_all x1, waiting for transfers between devices, local(): lax.all_to_all(level_all, SEQ, split_axis=0, concat_axis=2, tiled=True)  82.7 us
    all_gather x3, blocking collectives, gather_in_order(): pieces = lax.all_gather(pieces, axes[k], axis=0, tiled=True)  38.5 us
    all_to_all x1, starting transfers between devices, local(): lax.all_to_all(end_state.reshape(1, head_count * head_width, state_width)...  19.9 us
    select_n x6, other arithmetic, local(): jnp.where(is_upper[:, None, None], block_state + block_decay[:, :, None]...  19.1 us
    all_to_all x1, starting transfers between devices, local(): lax.all_to_all(level_all, SEQ, split_axis=0, concat_axis=2, tiled=True)  15.1 us
    dot_general x4, matrix products, head_group(): jnp.einsum('hts,shp->thp', mixing, group_scaled.reshape(tok_rows, group_s...  13.7 us
    all_to_all x1, blocking collectives, copy_for_each(): lax.all_to_all(jnp.broadcast_to(array[None], (size, *array.shape)), axis,...  9.58 us
    unnamed x7, other arithmetic  9.43 us
  transfers between devices with their start and end apart: 2, of which 1 were waited for; matrix products, arithmetic and copies ran while one was open for 6% of the time, Pallas kernels for 0%

commit v1 on v0

--- a/solution.py
+++ b/solution.py
@@ -1,8 +1,11 @@
+import functools
 import math
 
 import jax
 import jax.numpy as jnp
 from jax import lax
+from jax.experimental import pallas as pl
+from jax.experimental.pallas import tpu as pltpu
 from jax.sharding import Mesh
 from jax.sharding import PartitionSpec as P
 
@@ -13,26 +16,6 @@
 
 
 epsilon = 1e-06
-
-
-def joined_along(pieces, dim):
-    pieces = jnp.moveaxis(pieces, 0, dim)
-    shape = pieces.shape
-    return pieces.reshape(*shape[:dim], shape[dim] * shape[dim + 1], *shape[dim + 2 :])
-
-
-def gather_in_order(array, axes, turns):
-    pieces = array[None]
-    for k in turns:
-        pieces = lax.all_gather(pieces, axes[k], axis=0, tiled=True)
-    current = [lax.axis_size(axes[k]) for k in reversed(turns)]
-    pieces = pieces.reshape(*current, *array.shape)
-    turned = sorted(range(len(turns)), key=lambda place: turns[len(turns) - 1 - place])
-    return pieces.transpose(*turned, *range(len(turns), pieces.ndim)).reshape(-1, *array.shape)
-
-
-def gathered_by_axis(array, axes, turns, dim):
-    return joined_along(gather_in_order(array, axes, turns), dim)
 
 
 def copy_for_each(array, axis):
@@ -56,11 +39,256 @@
     return level_index
 
 
-def flip_pairs(tensor, bit_index):
-    split_view = tensor.reshape(
-        (tensor.shape[0] >> bit_index + 1, 2, 1 << bit_index) + tensor.shape[1:]
-    )
-    return split_view[:, ::-1].reshape(tensor.shape)
+MESH_ID = pl.DeviceIdType.MESH
+SHARD = 32
+
+
+def remote(src, dst, send, recv, where):
+    return pltpu.make_async_remote_copy(
+        src_ref=src, dst_ref=dst, send_sem=send, recv_sem=recv, device_id=where, device_id_type=MESH_ID
+    )
+
+
+def wait_bytes(ref, sem):
+    pltpu.make_async_copy(ref, ref, sem).wait()
+
+
+def lane_pick(rows, lane):
+    lanes = lax.broadcasted_iota(jnp.int32, rows.shape, 1)
+    return jnp.sum(jnp.where(lanes == lane, rows, 0.0), axis=1, keepdims=True)
+
+
+def levels_base(size, bits):
+    base, at = [], 0
+    for j in range(bits):
+        base.append(at)
+        at += size >> (j + 1)
+    return base, at
+
+
+def exchange_kernel(
+    nx, nz, e_ref, d_ref, rs_out, lead_out,
+    pe, pd, a_half, dc, inz, dz, outz, drow, xr, dxr, outx, rs,
+    pair_s, pair_r, z_s, z_r, x_s, x_r, lev_s, lev_r, fin_s, fin_r,
+):
+    bz, bx = nz.bit_length() - 1, nx.bit_length() - 1
+    base_z, total_z = levels_base(nz, bz)
+    base_x, _ = levels_base(nx, bx)
+    my_x, my_z, my_c = lax.axis_index("seq_0"), lax.axis_index("seq_1"), lax.axis_index("seq_2")
+    other = 1 - my_c
+    half_heads = nz * SHARD // 64
+
+    barrier = pltpu.get_barrier_semaphore()
+
+    def greet_z(o, c):
+        pl.semaphore_signal(barrier, inc=1, device_id={"seq_1": lax.rem(my_z + o, nz)}, device_id_type=MESH_ID)
+        return c
+
+    def greet_x(o, c):
+        pl.semaphore_signal(barrier, inc=1, device_id={"seq_0": lax.rem(my_x + o, nx)}, device_id_type=MESH_ID)
+        return c
+
+    pl.semaphore_signal(barrier, inc=1, device_id={"seq_2": other}, device_id_type=MESH_ID)
+    lax.fori_loop(1, nx, greet_x, 0)
+    lax.fori_loop(1, nz, greet_z, 0)
+    pl.semaphore_wait(barrier, nz + nx - 1)
+
+    ce = remote(e_ref, pe, pair_s.at[0], pair_r.at[0], {"seq_2": other})
+    cd = remote(d_ref, pd, pair_s.at[1], pair_r.at[1], {"seq_2": other})
+    ce.start()
+    cd.start()
+    cd.wait()
+    ce.wait()
+    first = my_c == 0
+    d_own, d_oth = d_ref[...], pd[...]
+    d0 = jnp.where(first, d_own, d_oth)
+    d1 = jnp.where(first, d_oth, d_own)
+    dc[...] = d0 * d1
+    for s in range(nz):
+        own = e_ref[my_c, s].astype(jnp.float32)
+        oth = pe[my_c, s].astype(jnp.float32)
+        e0 = jnp.where(first, own, oth)
+        e1 = jnp.where(first, oth, own)
+        scale = lane_pick(d1, my_c * half_heads + s * SHARD // 64)
+        a_half[s] = (e1 + scale * e0).astype(jnp.bfloat16)
+
+    def send_z(o, c):
+        to = lax.rem(my_z + o, nz)
+        remote(a_half.at[to], inz.at[my_z], z_s.at[0], z_r.at[0], {"seq_1": to}).start()
+        remote(dc, dz.at[my_z], z_s.at[1], z_r.at[1], {"seq_1": to}).start()
+        return c
+
+    lax.fori_loop(1, nz, send_z, 0)
+    inz[my_z] = a_half[my_z]
+    dz[my_z] = dc[...]
+    wait_bytes(dz.at[pl.ds(0, nz - 1)], z_r.at[1])
+    wait_bytes(inz.at[pl.ds(0, nz - 1)], z_r.at[0])
+
+    my_head = my_c * half_heads + my_z * SHARD // 64
+    rows_d = [dz[z] for z in range(nz)]
+    state = [inz[z].astype(jnp.float32) for z in range(nz)]
+    decay = [lane_pick(r, my_head) for r in rows_d]
+    for j in range(bz):
+        for m in range(0, nz >> j, 2):
+            outz[base_z[j] + m // 2] = state[m].astype(jnp.bfloat16)
+        state = [state[m + 1] + decay[m + 1] * state[m] for m in range(0, nz >> j, 2)]
+        decay = [decay[m + 1] * decay[m] for m in range(0, nz >> j, 2)]
+    outz[total_z] = state[0].astype(jnp.bfloat16)
+    row_product = rows_d[0]
+    for z in range(1, nz):
+        row_product = row_product * rows_d[z]
+    drow[...] = row_product
+
+    def send_x(o, c):
+        to = lax.rem(my_x + o, nx)
+        remote(outz.at[total_z], xr.at[my_x], x_s.at[0], x_r.at[0], {"seq_0": to}).start()
+        remote(drow, dxr.at[my_x], x_s.at[1], x_r.at[1], {"seq_0": to}).start()
+        return c
+
+    lax.fori_loop(1, nx, send_x, 0)
+    xr[my_x] = outz[total_z]
+    dxr[my_x] = drow[...]
+
+    def bit(value, j):
+        return lax.rem(value // (1 << j), 2) == 1
+
+    def send_levels_z(o, c):
+        to = lax.rem(my_z + o, nz)
+        for j in range(bz):
+            @pl.when(bit(to, j))
+            def _():
+                remote(
+                    outz.at[base_z[j] + to // (1 << (j + 1))], rs.at[j, my_c, my_z], lev_s.at[j], lev_r.at[j], {"seq_1": to}
+                ).start()
+        return c
+
+    lax.fori_loop(1, nz, send_levels_z, 0)
+    for j in range(bz):
+        @pl.when(bit(my_z, j))
+        def _():
+            rs[j, my_c, my_z] = outz[base_z[j] + my_z // (1 << (j + 1))]
+
+    wait_bytes(dxr.at[pl.ds(0, nx - 1)], x_r.at[1])
+    wait_bytes(xr.at[pl.ds(0, nx - 1)], x_r.at[0])
+    rows_x = [dxr[x] for x in range(nx)]
+    state = [xr[x].astype(jnp.float32) for x in range(nx)]
+    decay = [lane_pick(r, my_head) for r in rows_x]
+    for j in range(bx):
+        for m in range(0, nx >> j, 2):
+            outx[base_x[j] + m // 2] = state[m].astype(jnp.bfloat16)
+        state = [state[m + 1] + decay[m + 1] * state[m] for m in range(0, nx >> j, 2)]
+        decay = [decay[m + 1] * decay[m] for m in range(0, nx >> j, 2)]
+    for j in range(bx):
+        @pl.when(bit(my_x, j))
+        def _():
+            at = base_x[j] + my_x // (1 << (j + 1))
+
+            def send_levels_x(o, c):
+                to = lax.rem(my_z + o, nz)
+                remote(outx.at[at], rs.at[bz + j, my_c, my_z], lev_s.at[bz + j], lev_r.at[bz + j], {"seq_1": to}).start()
+                return c
+
+            lax.fori_loop(1, nz, send_levels_x, 0)
+            rs[bz + j, my_c, my_z] = outx[at]
+
+    one = jnp.ones_like(d0)
+    mine = jnp.where(first, one, d0)
+    lead_out[0] = one
+    for j in range(bz):
+        low = my_z // (1 << j) * (1 << j)
+        product = mine
+        for z in range(nz):
+            product = product * jnp.where((z >= low) & (z < my_z), rows_d[z], one)
+        lead_out[1 + j] = product
+    row_lead = mine
+    for z in range(nz):
+        row_lead = row_lead * jnp.where(z < my_z, rows_d[z], one)
+    for j in range(bx):
+        low = my_x // (1 << j) * (1 << j)
+        product = row_lead
+        for x in range(nx):
+            product = product * jnp.where((x >= low) & (x < my_x), rows_x[x], one)
+        lead_out[1 + bz + j] = product
+
+    flags = [bit(my_z, j) for j in range(bz)] + [bit(my_x, j) for j in range(bx)]
+    for v, flag in enumerate(flags):
+        @pl.when(flag)
+        def _():
+            wait_bytes(rs.at[v, 0, pl.ds(0, nz - 1)], lev_r.at[v])
+            remote(rs.at[v, my_c], rs.at[v, my_c], fin_s.at[v], fin_r.at[v], {"seq_2": other}).start()
+
+    @pl.when(first)
+    def _():
+        rs_out[0] = jnp.zeros_like(rs_out[0])
+
+    @pl.when(jnp.logical_not(first))
+    def _():
+        rs_out[0] = pe[...]
+
+    for v, flag in enumerate(flags):
+        @pl.when(flag)
+        def _():
+            remote(rs.at[v, my_c], rs.at[v, other], fin_s.at[v], fin_r.at[v], {"seq_2": other}).wait()
+            rs_out[1 + v] = rs[v]
+
+        @pl.when(jnp.logical_not(flag))
+        def _():
+            rs_out[1 + v] = jnp.zeros_like(rs[v])
+
+    wait_bytes(a_half.at[pl.ds(0, nz - 1)], z_s.at[0])
+    wait_bytes(dz.at[pl.ds(0, nz - 1)], z_s.at[1])
+    wait_bytes(xr.at[pl.ds(0, nx - 1)], x_s.at[0])
+    wait_bytes(dxr.at[pl.ds(0, nx - 1)], x_s.at[1])
+    for j in range(bz):
+        @pl.when(bit(my_z, j))
+        def _():
+            if nz // 2 > 1:
+                wait_bytes(inz.at[pl.ds(0, nz // 2 - 1)], lev_s.at[j])
+
+        @pl.when(jnp.logical_not(bit(my_z, j)))
+        def _():
+            wait_bytes(inz.at[pl.ds(0, nz // 2)], lev_s.at[j])
+    for j in range(bx):
+        @pl.when(bit(my_x, j))
+        def _():
+            wait_bytes(inz.at[pl.ds(0, nz - 1)], lev_s.at[bz + j])
+
+
+def exchange(end_state, span_decay, nx, nz):
+    rows, width = end_state.shape
+    heads = span_decay.shape[0]
+    levels = nz.bit_length() - 1 + nx.bit_length() - 1
+    vmem = pl.BlockSpec(memory_space=pltpu.VMEM)
+    bf, f32 = jnp.bfloat16, jnp.float32
+    dma = pltpu.SemaphoreType.DMA
+    states, leads = pl.pallas_call(
+        functools.partial(exchange_kernel, nx, nz),
+        name="exchange",
+        out_shape=(
+            jax.ShapeDtypeStruct((1 + levels, 2, nz, SHARD, width), bf),
+            jax.ShapeDtypeStruct((1 + levels, 1, 128), f32),
+        ),
+        in_specs=[vmem, vmem],
+        out_specs=(vmem, vmem),
+        scratch_shapes=[
+            pltpu.VMEM((2, nz, SHARD, width), bf),
+            pltpu.VMEM((1, 128), f32),
+            pltpu.VMEM((nz, SHARD, width), bf),
+            pltpu.VMEM((1, 128), f32),
+            pltpu.VMEM((nz, SHARD, width), bf),
+            pltpu.VMEM((nz, 1, 128), f32),
+            pltpu.VMEM((nz, SHARD, width), bf),
+            pltpu.VMEM((1, 128), f32),
+            pltpu.VMEM((nx, SHARD, width), bf),
+            pltpu.VMEM((nx, 1, 128), f32),
+            pltpu.VMEM((nx, SHARD, width), bf),
+            pltpu.VMEM((levels, 2, nz, SHARD, width), bf),
+            dma((2,)), dma((2,)), dma((2,)), dma((2,)), dma((2,)), dma((2,)),
+            dma((levels,)), dma((levels,)), dma((levels,)), dma((levels,)),
+        ],
+        compiler_params=pltpu.CompilerParams(collective_id=0, has_side_effects=True, vmem_limit_bytes=48 << 20),
+    )(end_state.reshape(2, nz, SHARD, width), jnp.pad(span_decay[None, :], ((0, 0), (0, 128 - heads))))
+    return states.reshape(1 + levels, rows, width), leads[:, 0, :heads]
 
 
 def local(
@@ -82,8 +310,7 @@
     state_width = key_proj.shape[1]
     per_span = doc_start.shape[0]
     low_bits = per_span.bit_length() - 1
-    span_total = lax.axis_size(SEQ)
-    span_bits = span_total.bit_length() - 1
+    span_bits = lax.axis_size(SEQ).bit_length() - 1
     table_rows = level_table.shape[0]
     level_count = level_table.shape[2]
     one_hot = (level_pick[:, None] == jnp.arange(table_rows, dtype=jnp.int32)[None, :]).astype(
@@ -111,50 +338,19 @@
     ).astype(jnp.bfloat16)
     end_state = jnp.einsum("sc,sn->cn", carried_in, key_proj, preferred_element_type=jnp.float32)
     span_decay = jnp.exp(end_log) * (doc_count[tok_rows - 1] == 0).astype(jnp.float32)
-    own_index = lax.axis_index(SEQ)
-    row_share = head_count * head_width // span_total
-    pieces = lax.all_to_all(
-        end_state.reshape(1, head_count * head_width, state_width).astype(jnp.bfloat16),
-        SEQ,
-        split_axis=1,
-        concat_axis=0,
-        tiled=True,
-    ).astype(jnp.float32)
-    decays = gathered_by_axis(span_decay.reshape(1, head_count), SEQ, (0, 1, 2), 0)
-    row_head = (own_index * row_share + jnp.arange(row_share, dtype=jnp.int32)) // head_width
-    head_pick = (row_head[:, None] == jnp.arange(head_count, dtype=jnp.int32)[None, :]).astype(
-        jnp.float32
-    )
-    block_decay = jnp.dot(
-        decays, head_pick.T, precision=lax.Precision.HIGHEST, preferred_element_type=jnp.float32
-    )
-    block_state = pieces
-    lead_decay = jnp.ones_like(block_decay)
-    span_range = jnp.arange(span_total, dtype=jnp.int32)
-    level_list = []
-    for bit_index in range(span_bits):
-        other_state = flip_pairs(block_state, bit_index)
-        other_decay = flip_pairs(block_decay, bit_index)
-        is_upper = span_range >> bit_index & 1 == 1
-        level_list.append(
-            jnp.where(is_upper[:, None, None], lead_decay[:, :, None] * other_state, 0.0)
-        )
-        block_state = jnp.where(
-            is_upper[:, None, None],
-            block_state + block_decay[:, :, None] * other_state,
-            other_state + other_decay[:, :, None] * block_state,
-        )
-        lead_decay = jnp.where(is_upper[:, None], lead_decay * other_decay, lead_decay)
-        block_decay = block_decay * other_decay
-    level_all = jnp.stack(level_list, 1).astype(jnp.bfloat16)
-    returned = lax.all_to_all(level_all, SEQ, split_axis=0, concat_axis=2, tiled=True)
-    remote_state = returned.reshape(span_bits, head_count, head_width, state_width)
+    states, leads = exchange(
+        end_state.astype(jnp.bfloat16), span_decay, lax.axis_size("seq_0"), lax.axis_size("seq_1")
+    )
+    remote_state = states.reshape(span_bits, head_count, head_width, state_width)
     level_index = level_of_pairs(tok_rows, STRETCH, low_bits)
     element_position = jnp.arange(tok_rows, dtype=jnp.int32)
     visible = (element_position[:, None] >= element_position[None, :]) & (
         doc_count[:, None] == doc_count[None, :]
     )
     scores = jnp.einsum("tn,sn->ts", query_proj, key_proj, preferred_element_type=jnp.float32)
+    level_weight = jnp.concatenate(
+        [level_weight[:, :, : 1 + low_bits], level_weight[:, :, 1 + low_bits :] * leads.T[None]], axis=2
+    )
     reach_decay = jnp.exp(log_total) * (doc_count == 0).astype(jnp.float32)[:, None]
     group_size = math.gcd(head_count, 4)
     group_count = head_count // group_size

time: 273 us -> 120 us (0.44)
  waiting for transfers between devices: 82.7 us -> 0 us
  Pallas kernels: 0 us -> 55.8 us
  blocking collectives: 48.1 us -> 9.6 us
  starting transfers between devices: 35 us -> 0 us
  other arithmetic: 46.5 us -> 12.9 us
  local copies, waits for them, and re-layouts: 33.5 us -> 18.7 us
    all_to_all x2 -> x0, waiting for transfers between devices: 82.7 us -> none  [the longest x1 82.7 us: local(): lax.all_to_all(level_all, SEQ, split_axis=0, concat_axis=2, tiled=True)]
    pallas_call x0 -> x1, Pallas kernels: none -> 55.8 us  [exchange(): pl.pallas_call(functools.partial(exchange_kernel, nx, nz), name='exchange...]
    all_gather x3 -> x0, blocking collectives: 38.5 us -> none  [gather_in_order(): pieces = lax.all_gather(pieces, axes[k], axis=0, tiled=True)]
    all_to_all x2 -> x0, starting transfers between devices: 35 us -> none  [the longest x1 19.9 us: local(): lax.all_to_all(end_state.reshape(1, head_count * head_width, state_width)...]
    select_n x8 -> x0, other arithmetic: 19.1 us -> none  [the longest x6 19.1 us: local(): jnp.where(is_upper[:, None, None], block_state + block_decay[:, :, None]...]
    unnamed x7 -> x0, other arithmetic: 9.43 us -> none
    rev x13 -> x0, local copies, waits for them, and re-layouts: 6.55 us -> none  [flip_pairs(): return split_view[:, ::-1].reshape(tensor.shape)]
    select_n x6 -> x0, local copies, waits for them, and re-layouts: 4.34 us -> none  [local(): jnp.where(is_upper[:, None], lead_decay * other_decay, lead_decay)]
  transfers between devices with their start and end apart: 2 -> 0, of which waited for: 1 -> 0; matrix products, arithmetic and copies ran while one was open for 6% -> 0% of each run, Pallas kernels for 0% -> 0%
where the time goes in v1:
time: 120 us; the launch traced here: 119 us
  Pallas kernels  55.8 us (46%)
  matrix products  21.4 us (18%)
  local copies, waits for them, and re-layouts  18.7 us (16%)
  other arithmetic  12.9 us (11%)
  blocking collectives  9.6 us (8%)
    pallas_call x1, Pallas kernels, exchange(): pl.pallas_call(functools.partial(exchange_kernel, nx, nz), name='exchange...  55.8 us
    dot_general x4, matrix products, head_group(): jnp.einsum('hts,shp->thp', mixing, group_scaled.reshape(tok_rows, group_s...  13.6 us
    all_to_all x1, blocking collectives, copy_for_each(): lax.all_to_all(jnp.broadcast_to(array[None], (size, *array.shape)), axis,...  9.6 us
    dot_general x4, matrix products, head_group(): jnp.einsum('tn,bhpn->tbhp', query_proj, group_remote, preferred_element_t...  6.8 us
    dynamic_slice x4, local copies, waits for them, and re-layouts, local(): group_parts = lax.map(head_group, stacked)  3.89 us
    eq x4, other arithmetic, head_group(): level_index[None] == level_id  3.76 us
    dynamic_update_slice x4, local copies, waits for them, and re-layouts, local(): group_parts = lax.map(head_group, stacked)  3.39 us
    unnamed x20, local copies, waits for them, and re-layouts  3.04 us

profile of v1, /device:TPU:6, one launch (start us, length us, event | category | flops | bytes accessed | tf_op | source)
XLA Modules:
  0.0 119.4 jit_solution(16829983346074120585)
XLA Ops:
  0.0 0.9 reduce-window.20
  0.9 0.1 broadcast_in_dim.120
  1.0 0.1 reshape.159
  1.1 0.6 slice.42
  2.3 0.6 compare_convert_fusion
  3.0 0.8 copy_bitcast_fusion.2
  3.8 1.1 reduce-window.18
  4.9 0.2 slice_reduce_fusion
  5.1 0.1 broadcast_add_fusion
  5.2 0.1 copy.62
  5.3 0.1 copy.66
  5.4 0.9 exponential_multiply_fusion
  6.3 0.1 copy.64
  6.4 0.5 copy.58
  7.0 0.0 copy-done.4
  7.0 0.0 copy-start.3
  7.0 0.0 copy-start.6
  7.0 1.3 %fusion.30 = (bf16[512,1024]{0,1:T(8,128)(2,1)S(1)}, bf16[512,1024]{0,1:T(8,128)(2,1)}) fusion(f32[512,16]{0,1:T(8,128)S(1)} %copy.64, bf16[512,1024]{0,1:T(8,128)(2,1)S(1)} %copy.58, f32[512,16]{0,1:T(8,128)S(1)} %copy-done.4), kind=kLoop, calls=%fused_computation.49 | loop fusion | flops 3145728 | bytes 3211264 | tf_op jit(solution)/shard_map/convert_element_type | solution.py:338
  8.4 0.4 convolution_convert_fusion
  8.8 55.8 %exchange.1 = (bf16[7,2,16,32,128]{4,3,2,1,0:T(8,128)(2,1)S(1)}, f32[7,1,128]{2,1,0:T(1,128)S(1)}) custom-call(bf16[2,16,32,128]{3,2,1,0:T(8,128)(2,1)S(1)} %bitcast.130, f32[1,128]{1,0:T(1,128)S(1)} %pad.4.d_ref), custom_call_target="tpu_custom_call" | custom-call | tf_op jit(solution)/shard_map/exchange/pallas_call | solution.py:264
  64.7 0.2 copy.59
  64.8 0.1 reshape.154
  64.9 0.1 dot_general.26
  65.1 0.2 copy.60
  65.2 0.3 fusion.32
  65.6 0.1 slice_multiply_fusion
  65.7 0.9 reshape.162
  66.5 1.0 copy.87
  67.6 0.0 copy-start.2
  67.6 1.4 %copy.86 = bf16[7,4,4,64,128]{4,3,2,0,1:T(8,128)(2,1)} copy(bf16[7,4,4,64,128]{4,3,2,1,0:T(8,128)(2,1)S(1)} %bitcast.129) | data formatting | bytes 3670016 | tf_op jit(solution)/shard_map/reshape;reshape;reshape | solution.py:389
  69.0 1.0 copy.67
  70.1 0.3 fusion.40
  70.4 32.6 %while.12 = (s32[]{:T(128)}, f32[4,512,256]{1,2,0:T(8,128)}, bf16[4,512,256]{1,2,0:T(8,128)(2,1)}, f32[512,512]{1,0:T(8,128)S(1)}, f32[4,512,4,11]{1,2,3,0:T(4,1...) while((s32[]{:T(128)}, f32[4,512,256]{1,2,0:T(8,128)}, ...), condition=%wide.region_4.5_spmd.clone.clone, body=%wide.region_3.4_spmd.clone.clone.sunk | while | flops 387842048 | bytes 8172673 | solution.py:394
  70.4 1.7 %fusion.60 = f32[512,4,64]{0,2,1:T(8,128)S(1)} fusion(f32[512,4,7]{0,1,2:T(4,128)S(1)} %slice.74, bf16[4,7,4,64,128]{4,3,2,1,0:T(8,128)(2,1)} %get-tuple-element.291, s32[]{:T(128)} %get-tuple-element.272, bf16[512,128]{1,0:T(8,128)(2,1)S(1)} %get-tuple-element.292), kind=kOutput, calls=%fused_computation.4.clone.1 | convolution fusion | flops 236584960 | bytes 1171968 | tf_op jit(solution)/shard_map/while/body/eval_jaxpr/tn,bhpn->tbhp/dot_general | solution.py:376
  72.2 1.0 constant_dynamic-slice_fusion.2
  73.2 0.9 fusion.59
  74.1 0.2 fusion.58
  74.3 3.4 %fusion.61 = f32[512,4,64]{0,2,1:T(8,128)S(1)} fusion(bf16[512,4,64]{0,2,1:T(8,128)(2,1)S(1)} %bitcast.133, f32[4,512]{1,0:T(4,128)S(1)} %get-tuple-element.250, f32[4,512]{1,0:T(4,128)S(1)} %get-tuple-element.251, f32[4,512]{1,0:T(4,128)S(1)} %get-tuple-element.252, f32[4,512]{1,0:T(4,128)S(1)} %get-tuple-element.253, ...), kind=kOutput, calls=%fused_computation.15.clone.1 | convolution fusion | flops 147062784 | bytes 3719168 | tf_op jit(solution)/shard_map/while/body/eval_jaxpr/hts,shp->thp/dot_general | solution.py:370
  77.7 0.8 constant_dynamic-update-slice_fusion.2
  78.6 1.7 %fusion.60 = f32[512,4,64]{0,2,1:T(8,128)S(1)} fusion(f32[512,4,7]{0,1,2:T(4,128)S(1)} %slice.74, bf16[4,7,4,64,128]{4,3,2,1,0:T(8,128)(2,1)} %get-tuple-element.291, s32[]{:T(128)} %get-tuple-element.272, bf16[512,128]{1,0:T(8,128)(2,1)S(1)} %get-tuple-element.292), kind=kOutput, calls=%fused_computation.4.clone.1 | convolution fusion | flops 236584960 | bytes 1171968 | tf_op jit(solution)/shard_map/while/body/eval_jaxpr/tn,bhpn->tbhp/dot_general | solution.py:376
  80.3 1.0 constant_dynamic-slice_fusion.2
  81.3 0.9 fusion.59
  82.2 0.2 fusion.58
  82.4 3.4 %fusion.61 = f32[512,4,64]{0,2,1:T(8,128)S(1)} fusion(bf16[512,4,64]{0,2,1:T(8,128)(2,1)S(1)} %bitcast.133, f32[4,512]{1,0:T(4,128)S(1)} %get-tuple-element.250, f32[4,512]{1,0:T(4,128)S(1)} %get-tuple-element.251, f32[4,512]{1,0:T(4,128)S(1)} %get-tuple-element.252, f32[4,512]{1,0:T(4,128)S(1)} %get-tuple-element.253, ...), kind=kOutput, calls=%fused_computation.15.clone.1 | convolution fusion | flops 147062784 | bytes 3719168 | tf_op jit(solution)/shard_map/while/body/eval_jaxpr/hts,shp->thp/dot_general | solution.py:370
  85.8 0.8 constant_dynamic-update-slice_fusion.2
  86.7 1.7 %fusion.60 = f32[512,4,64]{0,2,1:T(8,128)S(1)} fusion(f32[512,4,7]{0,1,2:T(4,128)S(1)} %slice.74, bf16[4,7,4,64,128]{4,3,2,1,0:T(8,128)(2,1)} %get-tuple-element.291, s32[]{:T(128)} %get-tuple-element.272, bf16[512,128]{1,0:T(8,128)(2,1)S(1)} %get-tuple-element.292), kind=kOutput, calls=%fused_computation.4.clone.1 | convolution fusion | flops 236584960 | bytes 1171968 | tf_op jit(solution)/shard_map/while/body/eval_jaxpr/tn,bhpn->tbhp/dot_general | solution.py:376
  88.4 1.0 constant_dynamic-slice_fusion.2
  89.4 0.9 fusion.59
  90.4 0.2 fusion.58
  90.6 3.4 %fusion.61 = f32[512,4,64]{0,2,1:T(8,128)S(1)} fusion(bf16[512,4,64]{0,2,1:T(8,128)(2,1)S(1)} %bitcast.133, f32[4,512]{1,0:T(4,128)S(1)} %get-tuple-element.250, f32[4,512]{1,0:T(4,128)S(1)} %get-tuple-element.251, f32[4,512]{1,0:T(4,128)S(1)} %get-tuple-element.252, f32[4,512]{1,0:T(4,128)S(1)} %get-tuple-element.253, ...), kind=kOutput, calls=%fused_computation.15.clone.1 | convolution fusion | flops 147062784 | bytes 3719168 | tf_op jit(solution)/shard_map/while/body/eval_jaxpr/hts,shp->thp/dot_general | solution.py:370
  94.0 0.9 constant_dynamic-update-slice_fusion.2
  94.9 1.7 %fusion.60 = f32[512,4,64]{0,2,1:T(8,128)S(1)} fusion(f32[512,4,7]{0,1,2:T(4,128)S(1)} %slice.74, bf16[4,7,4,64,128]{4,3,2,1,0:T(8,128)(2,1)} %get-tuple-element.291, s32[]{:T(128)} %get-tuple-element.272, bf16[512,128]{1,0:T(8,128)(2,1)S(1)} %get-tuple-element.292), kind=kOutput, calls=%fused_computation.4.clone.1 | convolution fusion | flops 236584960 | bytes 1171968 | tf_op jit(solution)/shard_map/while/body/eval_jaxpr/tn,bhpn->tbhp/dot_general | solution.py:376
  96.6 1.0 constant_dynamic-slice_fusion.2
  97.6 0.9 fusion.59
  98.5 0.2 fusion.58
  98.7 3.4 %fusion.61 = f32[512,4,64]{0,2,1:T(8,128)S(1)} fusion(bf16[512,4,64]{0,2,1:T(8,128)(2,1)S(1)} %bitcast.133, f32[4,512]{1,0:T(4,128)S(1)} %get-tuple-element.250, f32[4,512]{1,0:T(4,128)S(1)} %get-tuple-element.251, f32[4,512]{1,0:T(4,128)S(1)} %get-tuple-element.252, f32[4,512]{1,0:T(4,128)S(1)} %get-tuple-element.253, ...), kind=kOutput, calls=%fused_computation.15.clone.1 | convolution fusion | flops 147062784 | bytes 3719168 | tf_op jit(solution)/shard_map/while/body/eval_jaxpr/hts,shp->thp/dot_general | solution.py:370
  102.1 0.9 constant_dynamic-update-slice_fusion.2
  103.0 2.3 %copy.69 = bf16[512,1024]{0,1:T(8,128)(2,1)} copy(bf16[512,1024]{1,0:T(8,128)(2,1)} %param.14) | data formatting | bytes 2097152 | tf_op args[1]
  105.3 0.1 broadcast_in_dim.122
  105.3 0.1 mul.104
  105.4 2.8 %multiply_reduce_fusion = (f32[512]{0:T(512)S(1)}, f32[512,1024]{0,1:T(8,128)S(1)}) fusion(bf16[512,1024]{0,1:T(8,128)(2,1)} %copy.69, bf16[512,1024]{0,1:T(8,128)(2,1)S(1)} %copy.58, f32[1024]{0:T(1024)S(1)} %mul.104, f32[4,512,256]{1,2,0:T(8,128)} %get-tuple-element.75), kind=kLoop, calls=%fused_computation.51 | loop fusion | flops 5766656 | bytes 6297600 | tf_op jit(solution)/shard_map/reduce_sum | solution.py:400
  108.2 9.6 %all_to_all.6 = f32[4,1,512]{2,1,0:T(1,128)S(1)} all-to-all(f32[4,1,512]{2,1,0:T(1,128)S(1)} %broadcast_in_dim.123), channel_id=1, replica_groups=mesh['seq_0'=4,'seq_1'=16,'seq_2'=2,'head'=4] {'head'}, dimensions={0} | all-to-all | bytes 16384 | tf_op jit(solution)/shard_map/all_to_all | solution.py:23
  117.9 0.3 multiply_convert_fusion.6
  118.1 1.3 %copy.71 = bf16[512,1024]{1,0:T(8,128)(2,1)} copy(bf16[512,1024]{0,1:T(8,128)(2,1)S(1)} %multiply_convert_fusion.6) | data formatting | bytes 2097152 | tf_op jit(solution)/shard_map/convert_element_type | solution.py:402
  (42 shorter events, 0.3 us)
Async XLA Ops:
  0.0 8.4 %copy-start = (bf16[512,128]{1,0:T(8,128)(2,1)S(1)}, bf16[512,128]{1,0:T(8,128)(2,1)}, u32[]{:S(2)}) copy-start(bf16[512,128]{1,0:T(8,128)(2,1)} %param.15) | copy-start | bytes 393220
  0.0 6.4 %copy-start.1 = (bf16[512,1024]{1,0:T(8,128)(2,1)S(1)}, bf16[512,1024]{1,0:T(8,128)(2,1)}, u32[]{:S(2)}) copy-start(bf16[512,1024]{1,0:T(8,128)(2,1)} %param.13) | copy-start | bytes 3145732
  0.0 7.0 %copy-start.4 = (f32[512,16]{0,1:T(8,128)S(1)}, f32[512,16]{0,1:T(8,128)}, u32[]{:S(2)}) copy-start(f32[512,16]{0,1:T(8,128)} %param.17) | copy-start | bytes 98308
  7.0 57.6 %copy-start.3 = (f32[16,16,11]{1,0,2:T(8,128)S(1)}, f32[16,16,11]{1,0,2:T(8,128)}, u32[]{:S(2)}) copy-start(f32[16,16,11]{1,0,2:T(8,128)} %param.21) | copy-start | bytes 33796
  7.0 58.2 %copy-start.6 = (s32[512]{0:T(512)S(1)}, s32[512]{0:T(512)}, u32[]{:S(2)}) copy-start(s32[512]{0:T(512)} %param.22) | copy-start | bytes 6148
  67.6 2.5 %copy-start.2 = (bf16[512,128]{1,0:T(8,128)(2,1)S(1)}, bf16[512,128]{1,0:T(8,128)(2,1)}, u32[]{:S(2)}) copy-start(bf16[512,128]{1,0:T(8,128)(2,1)} %param.16) | copy-start | bytes 393220
  103.0 2.3 %copy-start.7 = (f32[16]{0:T(128)S(1)}, f32[16]{0:T(128)}, u32[]{:S(2)}) copy-start(f32[16]{0:T(128)} %param.19) | copy-start | bytes 196
  105.4 12.4 %copy-start.5 = (f32[1024]{0:T(1024)S(1)}, f32[1024]{0:T(1024)}, u32[]{:S(2)}) copy-start(f32[1024]{0:T(1024)} %param.20) | copy-start | bytes 12292

commit v2 on v1

v2 whole, which is shorter than its diff:
```python
import functools

import jax
import jax.numpy as jnp
from jax import lax
from jax.experimental import pallas as pl
from jax.experimental.pallas import tpu as pltpu
from jax.sharding import Mesh
from jax.sharding import PartitionSpec as P

HEADDIM = 64
STRETCH = 64
BLOCK = 256
SEQ = ("seq_0", "seq_1", "seq_2")
epsilon = 1e-06

MESH_ID = pl.DeviceIdType.MESH
SHARD = 32


def remote(src, dst, send, recv, where):
    return pltpu.make_async_remote_copy(
        src_ref=src, dst_ref=dst, send_sem=send, recv_sem=recv, device_id=where, device_id_type=MESH_ID
    )


def wait_bytes(ref, sem):
    pltpu.make_async_copy(ref, ref, sem).wait()


def lane_pick(rows, lane):
    lanes = lax.broadcasted_iota(jnp.int32, rows.shape, 1)
    return jnp.sum(jnp.where(lanes == lane, rows, 0.0), axis=1, keepdims=True)


def levels_base(size, bits):
    base, at = [], 0
    for j in range(bits):
        base.append(at)
        at += size >> (j + 1)
    return base, at


def bit(value, j):
    return lax.rem(value // (1 << j), 2) == 1


def nt_dot(a, b):
    return lax.dot_general(a, b, (((1,), (1,)), ((), ())), preferred_element_type=jnp.float32)


def layer_kernel(
    nx, nz, ny, val_hbm, gate_hbm, key_ref, query_ref, step_ref, log_ref, table_ref, pick_ref, doc_ref, skip_ref,
    gated_out, square_out,
    val_v, gate_v, val_t, scaled_t, var0, var1, var2, var3, rhs, acc_t, silu_t, steps, cuts, rows_s, rows_t,
    e_buf, d_buf, pe, pd, a_half, dc, inz, dz, outz, drow, xr, dxr, outx, rs, sq_own, sq,
    load_s, pair_s, pair_r, z_s, z_r, x_s, x_r, lev_s, lev_r, two_s, two_r, fin_s, fin_r, y_s, y_r,
):
    f32, bf = jnp.float32, jnp.bfloat16
    tok, ch = val_v.shape
    heads = ch // HEADDIM
    per_span = tok // STRETCH
    low_bits = per_span.bit_length() - 1
    bz, bx = nz.bit_length() - 1, nx.bit_length() - 1
    quads = nz // 4
    base_z, total_z = levels_base(nz, bz)
    base_x, _ = levels_base(nx, bx)
    my_x, my_z, my_c = lax.axis_index("seq_0"), lax.axis_index("seq_1"), lax.axis_index("seq_2")
    my_y = lax.axis_index("head")
    other = 1 - my_c
    half_heads = heads // 2

    def place(z):
        return lax.rem(z, 4) * quads + z // 4

    barrier = pltpu.get_barrier_semaphore()

    def greet(axis, mine, size):
        def step(o, c):
            pl.semaphore_signal(barrier, inc=1, device_id={axis: lax.rem(mine + o, size)}, device_id_type=MESH_ID)
            return c

        lax.fori_loop(1, size, step, 0)

    greet("seq_1", my_z, nz)
    greet("seq_0", my_x, nx)
    greet("head", my_y, ny)
    pl.semaphore_signal(barrier, inc=1, device_id={"seq_2": other}, device_id_type=MESH_ID)

    load_v = pltpu.make_async_copy(val_hbm, val_v, load_s.at[0])
    load_g = pltpu.make_async_copy(gate_hbm, gate_v, load_s.at[1])
    load_v.start()
    load_g.start()

    total = log_ref[...].T
    lane = lax.broadcasted_iota(jnp.int32, (heads, tok), 1)
    shift = 1
    while shift < tok:
        total = total + jnp.where(lane >= shift, pltpu.roll(total, shift, 1), 0.0)
        shift *= 2
    steps[...] = step_ref[...].T
    cuts[...] = total
    lane1 = lax.broadcasted_iota(jnp.int32, (1, tok), 1)
    count = doc_ref[0]
    docs = jnp.broadcast_to(count, (1, tok))
    for c in range(1, per_span):
        count = count + doc_ref[c]
        docs = jnp.where(lane1 >= c * STRETCH, count, docs)
    last = tok - 1
    end_log = total[:, last:]
    rows_s[0] = jnp.exp(end_log - total) * (docs == docs[:, last:]).astype(f32)
    square_mask = lax.broadcasted_iota(jnp.int32, (heads, 128), 0) == lax.broadcasted_iota(jnp.int32, (heads, 128), 1)
    end_decay = jnp.exp(end_log) * (docs[:, last:] == 0).astype(f32)
    d_buf[...] = jnp.sum(jnp.where(square_mask, end_decay, 0.0), axis=0, keepdims=True)

    load_v.wait()

    def end_pair(k, c):
        at = pl.multiple_of(k * 128, 128)
        v = val_v[:, pl.ds(at, 128)].astype(f32).T
        val_t[pl.ds(at, 128), :] = v.astype(bf)
        for i in range(2):
            h = 2 * k + i
            row = pl.ds(pl.multiple_of(h * HEADDIM, HEADDIM), HEADDIM)
            scaled = (v[i * HEADDIM : (i + 1) * HEADDIM] * steps[pl.ds(h, 1), :]).astype(bf)
            scaled_t[row, :] = scaled
            var0[row, :] = (scaled.astype(f32) * rows_s[0, pl.ds(h, 1), :]).astype(bf)
        return c

    lax.fori_loop(0, heads // 2, end_pair, 0)
    per = SHARD

    def end_dot(m, c):
        n = BLOCK // per
        part = jnp.dot(
            var0[pl.ds(pl.multiple_of(m * BLOCK, BLOCK), BLOCK), :], key_ref[...], preferred_element_type=f32
        ).astype(bf)
        for i in range(n):
            e_buf[m * n + i] = part[i * per : (i + 1) * per]
        return c

    lax.fori_loop(0, ch // BLOCK, end_dot, 0)

    pl.semaphore_wait(barrier, nz + nx + ny - 2)

    ce = remote(e_buf, pe, pair_s.at[0], pair_r.at[0], {"seq_2": other})
    cd = remote(d_buf, pd, pair_s.at[1], pair_r.at[1], {"seq_2": other})
    ce.start()
    cd.start()

    picks = jnp.broadcast_to(pick_ref[...], (heads, tok))
    levels = table_ref.shape[2]
    groups = table_ref.shape[0]
    for v in range(levels):
        w = jnp.zeros((heads, tok), f32)
        for g in range(groups):
            w = jnp.where(picks == g, table_ref[g, :, v : v + 1], w)
        rows_t[v] = w

    cd.wait()
    ce.wait()
    first = my_c == 0
    d_own, d_oth = d_buf[...], pd[...]
    d0 = jnp.where(first, d_own, d_oth)
    d1 = jnp.where(first, d_oth, d_own)
    dc[...] = d0 * d1

    def merge_pair(s, c):
        own = e_buf[my_c * nz + s].astype(f32)
        oth = pe[my_c * nz + s].astype(f32)
        e0 = jnp.where(first, own, oth)
        e1 = jnp.where(first, oth, own)
        scale = lane_pick(d1, my_c * half_heads + s * SHARD // HEADDIM)
        a_half[s] = (e1 + scale * e0).astype(bf)
        return c

    for s in range(nz):
        merge_pair(s, 0)

    def send_z(o, c):
        to = lax.rem(my_z + o, nz)
        remote(a_half.at[place(to)], inz.at[my_z], z_s.at[0], z_r.at[0], {"seq_1": to}).start()
        remote(dc, dz.at[my_z], z_s.at[1], z_r.at[1], {"seq_1": to}).start()
        return c

    lax.fori_loop(1, nz, send_z, 0)
    inz[my_z] = a_half[place(my_z)]
    dz[my_z] = dc[...]

    total = cuts[...]
    for v in range(low_bits + 1):
        width = STRETCH << max(v - 1, 0)
        mark, mark_doc = jnp.zeros((heads, tok), f32), jnp.zeros((1, tok), jnp.int32)
        if v == 0:
            for c in range(per_span):
                at = c * STRETCH + STRETCH // 2 - 1
                mark = jnp.where(lane >= c * STRETCH, total[:, at : at + 1], mark)
            rows_s[0] = jnp.exp(mark - total)
            rows_t[0] = rows_t[0] * jnp.exp(total - mark)
        else:
            for c in range(tok // (2 * width)):
                at = (2 * c + 1) * width - 1
                mark = jnp.where(lane >= 2 * c * width, total[:, at : at + 1], mark)
                mark_doc = jnp.where(lane1 >= 2 * c * width, docs[:, at : at + 1], mark_doc)
            upper = lane // width % 2 == 1
            same = (docs == mark_doc).astype(f32)
            rows_s[v] = jnp.where(upper, 0.0, jnp.exp(jnp.minimum(mark - total, 0.0)) * same)
            rows_t[v] = jnp.where(upper, rows_t[v] * jnp.exp(jnp.minimum(total - mark, 0.0)) * same, 0.0)
    reach = jnp.exp(total) * (docs == 0).astype(f32)
    for v in range(low_bits + 1, levels):
        rows_t[v] = rows_t[v] * reach

    source = lax.broadcasted_iota(jnp.int32, (BLOCK, BLOCK), 0)
    reader = lax.broadcasted_iota(jnp.int32, (BLOCK, BLOCK), 1)
    differ = jnp.bitwise_xor(source // STRETCH, reader // STRETCH)
    causal = source <= reader
    for b in range(tok // BLOCK):
        part = slice(b * BLOCK, (b + 1) * BLOCK)
        scores = jnp.where(causal, nt_dot(key_ref[part, :], query_ref[part, :]), 0.0)
        rhs[3 * b] = jnp.where(differ == 0, scores, 0.0).astype(bf)
        rhs[3 * b + 1] = jnp.where(differ == 1, scores, 0.0).astype(bf)
        rhs[3 * b + 2] = jnp.where(differ >= 2, scores, 0.0).astype(bf)
    rhs[6] = nt_dot(key_ref[:BLOCK, :], query_ref[BLOCK:, :]).astype(bf)

    def variants(h, c):
        row = pl.ds(pl.multiple_of(h * HEADDIM, HEADDIM), HEADDIM)
        scaled = scaled_t[row, :].astype(f32)
        var0[row, :] = (scaled * rows_s[0, pl.ds(h, 1), :]).astype(bf)
        var1[row, :] = (scaled * rows_s[1, pl.ds(h, 1), :]).astype(bf)
        var2[row, :] = (scaled * rows_s[2, pl.ds(h, 1), :]).astype(bf)
        var3[row, :] = (scaled[:, :BLOCK] * rows_s[3, pl.ds(h, 1), :BLOCK]).astype(bf)
        return c

    lax.fori_loop(0, heads, variants, 0)
    per_block = BLOCK // HEADDIM

    def inner(m, c):
        row = pl.ds(pl.multiple_of(m * BLOCK, BLOCK), BLOCK)
        for b in range(tok // BLOCK):
            part = slice(b * BLOCK, (b + 1) * BLOCK)
            products = [
                jnp.dot(var[row, part], rhs[3 * b + v], preferred_element_type=f32)
                for v, var in enumerate((var0, var1, var2))
            ]
            if b:
                products.append(jnp.dot(var3[row, :], rhs[6], preferred_element_type=f32))
            for i in range(per_block):
                h = m * per_block + i
                own = slice(i * HEADDIM, (i + 1) * HEADDIM)
                at = pl.ds(pl.multiple_of(h * HEADDIM, HEADDIM), HEADDIM)
                out = skip_ref[h] * val_t[at, part].astype(f32)
                for v, product in enumerate(products):
                    out = out + rows_t[v, pl.ds(h, 1), part] * product[own]
                acc_t[at, part] = out
        return c

    lax.fori_loop(0, ch // BLOCK, inner, 0)

    wait_bytes(dz.at[pl.ds(0, nz - 1)], z_r.at[1])
    wait_bytes(inz.at[pl.ds(0, nz - 1)], z_r.at[0])
    my_head = my_c * half_heads + place(my_z) * SHARD // HEADDIM
    rows_d = [dz[z] for z in range(nz)]
    state = [inz[z].astype(f32) for z in range(nz)]
    decay = [lane_pick(r, my_head) for r in rows_d]
    for j in range(bz):
        for m in range(0, nz >> j, 2):
            outz[base_z[j] + m // 2] = state[m].astype(bf)
        state = [state[m + 1] + decay[m + 1] * state[m] for m in range(0, nz >> j, 2)]
        decay = [decay[m + 1] * decay[m] for m in range(0, nz >> j, 2)]
    outz[total_z] = state[0].astype(bf)
    row_product = rows_d[0]
    for z in range(1, nz):
        row_product = row_product * rows_d[z]
    drow[...] = row_product

    def send_x(o, c):
        to = lax.rem(my_x + o, nx)
        remote(outz.at[total_z], xr.at[my_x], x_s.at[0], x_r.at[0], {"seq_0": to}).start()
        remote(drow, dxr.at[my_x], x_s.at[1], x_r.at[1], {"seq_0": to}).start()
        return c

    lax.fori_loop(1, nx, send_x, 0)
    xr[my_x] = outz[total_z]
    dxr[my_x] = drow[...]

    def send_levels_z(wanted):
        def step(o, c):
            to = lax.rem(my_z + o, nz)
            for j in wanted:
                @pl.when(bit(to, j))
                def _():
                    remote(
                        outz.at[base_z[j] + to // (1 << (j + 1))], rs.at[j, my_c, place(my_z)],
                        lev_s.at[j], lev_r.at[j], {"seq_1": to},
                    ).start()
            return c

        lax.fori_loop(1, nz, step, 0)
        for j in wanted:
            @pl.when(bit(my_z, j))
            def _():
                rs[j, my_c, place(my_z)] = outz[base_z[j] + my_z // (1 << (j + 1))]

    send_levels_z(range(bz // 2, bz))

    one = jnp.ones_like(d0)
    mine = jnp.where(first, one, d0)

    def weigh(v, lead):
        column = jnp.sum(jnp.where(square_mask, lead, 0.0), axis=1, keepdims=True)
        rows_t[v] = rows_t[v] * column

    for j in range(bz):
        low = my_z // (1 << j) * (1 << j)
        product = mine
        for z in range(nz):
            product = product * jnp.where((z >= low) & (z < my_z), rows_d[z], one)
        weigh(low_bits + 2 + j, product)
    row_lead = mine
    for z in range(nz):
        row_lead = row_lead * jnp.where(z < my_z, rows_d[z], one)

    wait_bytes(dxr.at[pl.ds(0, nx - 1)], x_r.at[1])
    wait_bytes(xr.at[pl.ds(0, nx - 1)], x_r.at[0])
    rows_x = [dxr[x] for x in range(nx)]
    state = [xr[x].astype(f32) for x in range(nx)]
    decay = [lane_pick(r, my_head) for r in rows_x]
    for j in range(bx):
        for m in range(0, nx >> j, 2):
            outx[base_x[j] + m // 2] = state[m].astype(bf)
        state = [state[m + 1] + decay[m + 1] * state[m] for m in range(0, nx >> j, 2)]
        decay = [decay[m + 1] * decay[m] for m in range(0, nx >> j, 2)]
    for j in range(bx):
        @pl.when(bit(my_x, j))
        def _():
            at = base_x[j] + my_x // (1 << (j + 1))
            for o in range(1, quads):
                to = lax.rem(my_z + 4 * o, nz)
                remote(
                    outx.at[at], rs.at[bz + j, my_c, place(my_z)], lev_s.at[bz + j], lev_r.at[bz + j], {"seq_1": to}
                ).start()
            rs[bz + j, my_c, place(my_z)] = outx[at]

    send_levels_z(range(bz // 2))
    for j in range(bx):
        low = my_x // (1 << j) * (1 << j)
        product = row_lead
        for x in range(nx):
            product = product * jnp.where((x >= low) & (x < my_x), rows_x[x], one)
        weigh(low_bits + 2 + bz + j, product)

    load_g.wait()

    def gate_pair(k, c):
        at = pl.multiple_of(k * 128, 128)
        g = gate_v[:, pl.ds(at, 128)].astype(f32)
        silu_t[pl.ds(at, 128), :] = (g / (1.0 + jnp.exp(-g))).T
        return c

    lax.fori_loop(0, heads // 2, gate_pair, 0)

    residue = lax.rem(my_z, 4) * quads
    for j in range(bx):
        @pl.when(bit(my_x, j))
        def _():
            if quads > 1:
                wait_bytes(rs.at[bz + j, 0, pl.ds(0, quads - 1)], lev_r.at[bz + j])
            for o in (1, nz - 1, 2):
                part = rs.at[bz + j, my_c, pl.ds(residue, quads)]
                remote(part, part, two_s.at[j], two_r.at[j], {"seq_1": lax.rem(my_z + o, nz)}).start()

    def apply(v, ref, rows):
        def step(m, c):
            for b in range(tok // BLOCK):
                part = slice(b * BLOCK, (b + 1) * BLOCK)
                block = ref(m)
                product = nt_dot(block, query_ref[part, :])
                for i in range(per_block):
                    h = m * per_block + i
                    at = pl.ds(pl.multiple_of(h * HEADDIM, HEADDIM), HEADDIM)
                    acc_t[at, part] += rows_t[v, pl.ds(h, 1), part] * product[i * HEADDIM : (i + 1) * HEADDIM]
            return c

        lax.fori_loop(rows[0], rows[1], step, 0)

    chunks = ch // BLOCK
    n = BLOCK // SHARD
    half_chunks = chunks // 2

    @pl.when(jnp.logical_not(first))
    def _():
        apply(low_bits + 1, lambda m: pe[pl.ds(m * n, n)].reshape(BLOCK, 128), (0, chunks))

    def swap(v):
        return remote(rs.at[v, my_c], rs.at[v, my_c], fin_s.at[v], fin_r.at[v], {"seq_2": other})

    def level_block(v):
        if half_chunks:
            return lambda m: rs[v, m // half_chunks, pl.ds(lax.rem(m, half_chunks) * n, n)].reshape(BLOCK, 128)
        return lambda m: jnp.concatenate([rs[v, 0].reshape(BLOCK // 2, 128), rs[v, 1].reshape(BLOCK // 2, 128)])

    for j in reversed(range(bz)):
        @pl.when(bit(my_z, j))
        def _():
            wait_bytes(rs.at[j, 0, pl.ds(0, nz - 1)], lev_r.at[j])
            swap(j).start()

    for j in reversed(range(bz)):
        @pl.when(bit(my_z, j))
        def _():
            swap(j).wait()
            apply(low_bits + 2 + j, level_block(j), (0, chunks))

    for j in range(bx):
        @pl.when(bit(my_x, j))
        def _():
            wait_bytes(rs.at[bz + j, 0, pl.ds(0, 3 * quads)], two_r.at[j])
            swap(bz + j).start()

    for j in range(bx):
        @pl.when(bit(my_x, j))
        def _():
            v = bz + j
            if half_chunks:
                apply(low_bits + 2 + v, level_block(v), (my_c * half_chunks, (my_c + 1) * half_chunks))
                swap(v).wait()
                apply(low_bits + 2 + v, level_block(v), (other * half_chunks, (other + 1) * half_chunks))
            else:
                swap(v).wait()
                apply(low_bits + 2 + v, level_block(v), (0, chunks))

    def gate_rows(k, squares):
        row = pl.ds(pl.multiple_of(k * 128, 128), 128)
        g = acc_t[row, :] * silu_t[row, :]
        acc_t[row, :] = g
        return squares + jnp.sum(g * g, axis=0, keepdims=True)

    sq_own[...] = lax.fori_loop(0, heads // 2, gate_rows, jnp.zeros((1, tok), f32))

    def send_y(o, c):
        remote(sq_own, sq.at[my_y], y_s, y_r, {"head": lax.rem(my_y + o, ny)}).start()
        return c

    lax.fori_loop(1, ny, send_y, 0)
    sq[my_y] = sq_own[...]

    def back(k, c):
        at = pl.multiple_of(k * 128, 128)
        gated_out[:, pl.ds(at, 128)] = acc_t[pl.ds(at, 128), :].T
        return c

    lax.fori_loop(0, heads // 2, back, 0)

    wait_bytes(a_half.at[pl.ds(0, nz - 1)], z_s.at[0])
    wait_bytes(dz.at[pl.ds(0, nz - 1)], z_s.at[1])
    wait_bytes(xr.at[pl.ds(0, nx - 1)], x_s.at[0])
    wait_bytes(dxr.at[pl.ds(0, nx - 1)], x_s.at[1])
    for j in range(bz):
        @pl.when(bit(my_z, j))
        def _():
            if nz // 2 > 1:
                wait_bytes(inz.at[pl.ds(0, nz // 2 - 1)], lev_s.at[j])

        @pl.when(jnp.logical_not(bit(my_z, j)))
        def _():
            wait_bytes(inz.at[pl.ds(0, nz // 2)], lev_s.at[j])
    for j in range(bx):
        @pl.when(bit(my_x, j))
        def _():
            if quads > 1:
                wait_bytes(inz.at[pl.ds(0, quads - 1)], lev_s.at[bz + j])
            wait_bytes(rs.at[bz + j, 0, pl.ds(0, 3 * quads)], two_s.at[j])
    if ny > 1:
        wait_bytes(sq.at[pl.ds(0, ny - 1)], y_s)
        wait_bytes(sq.at[pl.ds(0, ny - 1)], y_r)
    squares = sq[0]
    for y in range(1, ny):
        squares = squares + sq[y]
    square_out[...] = squares


def local(
    values_in, gate_in, key_proj, query_proj, step_size, log_decay, skip_weight, norm_gain, level_table, level_pick, doc_start,
):
    nx, nz, ny = lax.axis_size("seq_0"), lax.axis_size("seq_1"), lax.axis_size("head")
    tok, ch = values_in.shape
    heads = step_size.shape[1]
    width = key_proj.shape[1]
    levels_out = nz.bit_length() - 1 + nx.bit_length() - 1
    bx = nx.bit_length() - 1
    table_levels = level_table.shape[2]
    bf, f32 = jnp.bfloat16, jnp.float32
    vmem = pl.BlockSpec(memory_space=pltpu.VMEM)
    smem = pl.BlockSpec(memory_space=pltpu.SMEM)
    hbm = pl.BlockSpec(memory_space=pl.ANY)
    dma = pltpu.SemaphoreType.DMA
    V = pltpu.VMEM
    gated, squares = pl.pallas_call(
        functools.partial(layer_kernel, nx, nz, ny),
        name="layer",
        out_shape=(jax.ShapeDtypeStruct((tok, ch), f32), jax.ShapeDtypeStruct((1, tok), f32)),
        in_specs=[hbm, hbm, vmem, vmem, vmem, vmem, vmem, vmem, smem, smem],
        out_specs=(vmem, vmem),
        scratch_shapes=[
            V((tok, ch), bf), V((tok, ch), bf), V((ch, tok), bf), V((ch, tok), bf),
            V((ch, tok), bf), V((ch, tok), bf), V((ch, tok), bf), V((ch, BLOCK), bf),
            V((7, BLOCK, BLOCK), bf), V((ch, tok), f32), V((ch, tok), f32),
            V((heads, tok), f32), V((heads, tok), f32), V((4, heads, tok), f32), V((table_levels, heads, tok), f32),
            V((2 * nz, SHARD, width), bf), V((1, 128), f32), V((2 * nz, SHARD, width), bf), V((1, 128), f32),
            V((nz, SHARD, width), bf), V((1, 128), f32), V((nz, SHARD, width), bf), V((nz, 1, 128), f32),
            V((nz, SHARD, width), bf), V((1, 128), f32), V((nx, SHARD, width), bf), V((nx, 1, 128), f32),
            V((nx, SHARD, width), bf), V((levels_out, 2, nz, SHARD, width), bf),
            V((1, tok), f32), V((ny, 1, tok), f32),
            dma((2,)), dma((2,)), dma((2,)), dma((2,)), dma((2,)), dma((2,)), dma((2,)),
            dma((levels_out,)), dma((levels_out,)), dma((bx,)), dma((bx,)), dma((levels_out,)), dma((levels_out,)),
            dma, dma,
        ],
        compiler_params=pltpu.CompilerParams(collective_id=0, has_side_effects=True, vmem_limit_bytes=50 << 20),
    )(
        values_in, gate_in, key_proj, query_proj, step_size, log_decay, level_table, level_pick.reshape(1, tok),
        doc_start, skip_weight,
    )
    mean_square = squares[0] / (ch * ny)
    return (gated * lax.rsqrt(mean_square + epsilon)[:, None] * norm_gain[None, :]).astype(bf)


def solution(mesh):
    split = Mesh(
        mesh.devices.reshape(4, 16, 2, mesh.shape["head"]), ("seq_0", "seq_1", "seq_2", "head")
    )
    return on_mesh(split)


def on_mesh(split):
    placed = (
        P(SEQ, "head"),
        P(SEQ, "head"),
        P(SEQ, None),
        P(SEQ, None),
        P(SEQ, "head"),
        P(SEQ, "head"),
        P("head"),
        P("head"),
        P(None, "head", None),
        P(SEQ),
        P(SEQ),
    )
    return jax.shard_map(local, mesh=split, in_specs=placed, out_specs=P(SEQ, "head"), check_vma=False)
```

time: 120 us -> 73.8 us (0.61)
  the two profiles are of different devices: /device:TPU:6 before, /device:TPU:38 now
where the time goes in v2:
time: 73.8 us; the launch traced here: 73.3 us
  Pallas kernels  61.4 us (83%)
  local copies, waits for them, and re-layouts  9.08 us (12%)
  other arithmetic  2.81 us (4%)
    pallas_call x1, Pallas kernels, local(): pl.pallas_call(functools.partial(layer_kernel, nx, nz, ny), name='layer',...  61.4 us
    unnamed x19, local copies, waits for them, and re-layouts  9.08 us
    convert_element_type x1, other arithmetic, local(): (gated * lax.rsqrt(mean_square + epsilon)[:, None] * norm_gain[None, :])....  2.8 us

profile of v2, /device:TPU:38, one launch (start us, length us, event | category | flops | bytes accessed | tf_op | source)
XLA Modules:
  0.0 73.3 jit_solution(1155052998934495410)
XLA Ops:
  0.0 0.0 copy-start.7
  0.0 1.1 %copy.14.table_ref = f32[16,16,11]{2,1,0:T(8,128)S(1)} copy(f32[16,16,11]{1,0,2:T(8,128)} %param.19) | data formatting | bytes 22528 | tf_op args[8]
  1.1 0.9 %copy.12.step_ref = f32[512,16]{1,0:T(8,128)S(1)} copy(f32[512,16]{0,1:T(8,128)} %param.15) | data formatting | bytes 65536 | tf_op args[4]
  2.0 0.9 %copy.13.log_ref = f32[512,16]{1,0:T(8,128)S(1)} copy(f32[512,16]{0,1:T(8,128)} %param.16) | data formatting | bytes 65536 | tf_op args[5]
  2.8 0.0 copy-start
  2.9 1.2 %copy-done = bf16[512,1024]{1,0:T(8,128)(2,1)S(1)} copy-done((bf16[512,1024]{1,0:T(8,128)(2,1)S(1)}, bf16[512,1024]{1,0:T(8,128)(2,1)}, u32[]{:S(2)}) %copy-start) | copy-done | bytes 1048600
  4.1 0.0 copy-start.1
  4.1 1.2 %copy-done.1 = bf16[512,1024]{1,0:T(8,128)(2,1)S(1)} copy-done((bf16[512,1024]{1,0:T(8,128)(2,1)S(1)}, bf16[512,1024]{1,0:T(8,128)(2,1)}, u32[]{:S(2)}) %copy-start.1) | copy-done | bytes 1048600
  5.3 0.0 copy-start.2
  5.3 0.9 %copy-done.2 = bf16[512,128]{1,0:T(8,128)(2,1)S(1)} copy-done((bf16[512,128]{1,0:T(8,128)(2,1)S(1)}, bf16[512,128]{1,0:T(8,128)(2,1)}, u32[]{:S(2)}) %copy-start.2) | copy-done | bytes 131096
  6.2 0.0 copy-start.3
  6.2 0.9 %copy-done.3 = bf16[512,128]{1,0:T(8,128)(2,1)S(1)} copy-done((bf16[512,128]{1,0:T(8,128)(2,1)S(1)}, bf16[512,128]{1,0:T(8,128)(2,1)}, u32[]{:S(2)}) %copy-start.3) | copy-done | bytes 131096
  7.1 0.0 copy-start.4
  7.1 0.7 copy-done.4
  7.8 0.0 copy-start.5
  7.8 0.7 copy-done.5
  8.5 0.0 copy-start.6
  8.5 0.7 copy-done.6
  9.1 61.4 %layer.1 = (f32[512,1024]{1,0:T(8,128)}, f32[1,512]{1,0:T(1,128)S(1)}) custom-call(bf16[512,1024]{1,0:T(8,128)(2,1)S(1)} %copy-done, bf16[512,1024]{1,0:T(8,128)(2,1)S(1)} %copy-done.1, bf16[512,128]{1,0:T(8,128)(2,1)S(1)} %copy-done.2, bf16[512,128]{1,0:T(8,128)(2,1)S(1)} %copy-done.3, f32[512,16]{1,0:T(8,128)S(1)} %copy.12.step_ref, ...), custom_call_target="tpu_custom_call" | custom-call | tf_op jit(solution)/shard_map/layer/pallas_call | solution.py:498
  70.5 0.0 copy-done.7
  70.5 2.8 %multiply_convert_fusion = bf16[512,1024]{1,0:T(8,128)(2,1)} fusion(f32[512,1024]{1,0:T(8,128)} %get-tuple-element.7, f32[1024]{0:T(1024)S(1)} %copy-done.7, f32[512]{0:T(512)S(1)} %bitcast.3), kind=kLoop, calls=%fused_computation | loop fusion | flops 1572864 | bytes 3151872 | tf_op jit(solution)/shard_map/convert_element_type | solution.py:524
  (1 shorter events, 0.0 us)
Async XLA Ops:
  0.0 70.5 %copy-start.7 = (f32[1024]{0:T(1024)S(1)}, f32[1024]{0:T(1024)}, u32[]{:S(2)}) copy-start(f32[1024]{0:T(1024)} %param.18) | copy-start | bytes 12292
  2.8 1.2 %copy-start = (bf16[512,1024]{1,0:T(8,128)(2,1)S(1)}, bf16[512,1024]{1,0:T(8,128)(2,1)}, u32[]{:S(2)}) copy-start(bf16[512,1024]{1,0:T(8,128)(2,1)} %val_hbm.1) | copy-start | bytes 3145732
  4.1 1.2 %copy-start.1 = (bf16[512,1024]{1,0:T(8,128)(2,1)S(1)}, bf16[512,1024]{1,0:T(8,128)(2,1)}, u32[]{:S(2)}) copy-start(bf16[512,1024]{1,0:T(8,128)(2,1)} %gate_hbm.1) | copy-start | bytes 3145732
  5.3 0.9 %copy-start.2 = (bf16[512,128]{1,0:T(8,128)(2,1)S(1)}, bf16[512,128]{1,0:T(8,128)(2,1)}, u32[]{:S(2)}) copy-start(bf16[512,128]{1,0:T(8,128)(2,1)} %key_ref.1) | copy-start | bytes 393220
  6.2 0.9 %copy-start.3 = (bf16[512,128]{1,0:T(8,128)(2,1)S(1)}, bf16[512,128]{1,0:T(8,128)(2,1)}, u32[]{:S(2)}) copy-start(bf16[512,128]{1,0:T(8,128)(2,1)} %query_ref.1) | copy-start | bytes 393220
  7.1 0.7 copy-start.4
  7.8 0.7 copy-start.5
  8.5 0.7 copy-start.6

commit v3 on v2

--- a/solution.py
+++ b/solution.py
@@ -50,8 +50,9 @@
 
 
 def layer_kernel(
-    nx, nz, ny, val_hbm, gate_hbm, key_ref, query_ref, step_ref, log_ref, table_ref, pick_ref, doc_ref, skip_ref,
+    nx, nz, ny, val_hbm, gate_hbm, key_hbm, query_hbm, step_hbm, log_hbm, table_hbm, pick_hbm, doc_hbm, skip_hbm,
     gated_out, square_out,
+    key_ref, query_ref, log_ref, table_ref, pick_ref, doc_ref, skip_ref,
     val_v, gate_v, val_t, scaled_t, var0, var1, var2, var3, rhs, acc_t, silu_t, steps, cuts, rows_s, rows_t,
     e_buf, d_buf, pe, pd, a_half, dc, inz, dz, outz, drow, xr, dxr, outx, rs, sq_own, sq,
     load_s, pair_s, pair_r, z_s, z_r, x_s, x_r, lev_s, lev_r, two_s, two_r, fin_s, fin_r, y_s, y_r,
@@ -87,18 +88,24 @@
     greet("head", my_y, ny)
     pl.semaphore_signal(barrier, inc=1, device_id={"seq_2": other}, device_id_type=MESH_ID)
 
-    load_v = pltpu.make_async_copy(val_hbm, val_v, load_s.at[0])
-    load_g = pltpu.make_async_copy(gate_hbm, gate_v, load_s.at[1])
-    load_v.start()
-    load_g.start()
-
-    total = log_ref[...].T
+    loads = [
+        pltpu.make_async_copy(src, dst, load_s.at[i])
+        for i, (src, dst) in enumerate((
+            (log_hbm, log_ref), (doc_hbm, doc_ref), (val_hbm, val_v), (step_hbm, steps), (key_hbm, key_ref),
+            (query_hbm, query_ref), (table_hbm, table_ref), (pick_hbm, pick_ref), (skip_hbm, skip_ref), (gate_hbm, gate_v),
+        ))
+    ]
+    for load in loads:
+        load.start()
+    loads[0].wait()
+    loads[1].wait()
+
+    total = log_ref[...]
     lane = lax.broadcasted_iota(jnp.int32, (heads, tok), 1)
     shift = 1
     while shift < tok:
         total = total + jnp.where(lane >= shift, pltpu.roll(total, shift, 1), 0.0)
         shift *= 2
-    steps[...] = step_ref[...].T
     cuts[...] = total
     lane1 = lax.broadcasted_iota(jnp.int32, (1, tok), 1)
     count = doc_ref[0]
@@ -113,7 +120,8 @@
     end_decay = jnp.exp(end_log) * (docs[:, last:] == 0).astype(f32)
     d_buf[...] = jnp.sum(jnp.where(square_mask, end_decay, 0.0), axis=0, keepdims=True)
 
-    load_v.wait()
+    for load in loads[2:5]:
+        load.wait()
 
     def end_pair(k, c):
         at = pl.multiple_of(k * 128, 128)
@@ -148,13 +156,15 @@
     ce.start()
     cd.start()
 
+    for load in loads[5:9]:
+        load.wait()
     picks = jnp.broadcast_to(pick_ref[...], (heads, tok))
-    levels = table_ref.shape[2]
-    groups = table_ref.shape[0]
+    levels, groups, _ = table_ref.shape
     for v in range(levels):
         w = jnp.zeros((heads, tok), f32)
+        columns = table_ref[v].T
         for g in range(groups):
-            w = jnp.where(picks == g, table_ref[g, :, v : v + 1], w)
+            w = jnp.where(picks == g, columns[:, g : g + 1], w)
         rows_t[v] = w
 
     cd.wait()
@@ -349,7 +359,7 @@
             product = product * jnp.where((x >= low) & (x < my_x), rows_x[x], one)
         weigh(low_bits + 2 + bz + j, product)
 
-    load_g.wait()
+    loads[9].wait()
 
     def gate_pair(k, c):
         at = pl.multiple_of(k * 128, 128)
@@ -446,7 +456,7 @@
 
     def back(k, c):
         at = pl.multiple_of(k * 128, 128)
-        gated_out[:, pl.ds(at, 128)] = acc_t[pl.ds(at, 128), :].T
+        gated_out[:, pl.ds(at, 128)] = acc_t[pl.ds(at, 128), :].T.astype(bf)
         return c
 
     lax.fori_loop(0, heads // 2, back, 0)
@@ -491,17 +501,18 @@
     table_levels = level_table.shape[2]
     bf, f32 = jnp.bfloat16, jnp.float32
     vmem = pl.BlockSpec(memory_space=pltpu.VMEM)
-    smem = pl.BlockSpec(memory_space=pltpu.SMEM)
-    hbm = pl.BlockSpec(memory_space=pl.ANY)
+    hbm = pl.BlockSpec(memory_space=pltpu.HBM)
     dma = pltpu.SemaphoreType.DMA
     V = pltpu.VMEM
     gated, squares = pl.pallas_call(
         functools.partial(layer_kernel, nx, nz, ny),
         name="layer",
-        out_shape=(jax.ShapeDtypeStruct((tok, ch), f32), jax.ShapeDtypeStruct((1, tok), f32)),
-        in_specs=[hbm, hbm, vmem, vmem, vmem, vmem, vmem, vmem, smem, smem],
+        out_shape=(jax.ShapeDtypeStruct((tok, ch), bf), jax.ShapeDtypeStruct((1, tok), f32)),
+        in_specs=[hbm] * 10,
         out_specs=(vmem, vmem),
         scratch_shapes=[
+            V((tok, width), bf), V((tok, width), bf), V((heads, tok), f32), V((table_levels, level_table.shape[0], heads), f32),
+            V((1, tok), jnp.int32), pltpu.SMEM((doc_start.shape[0],), jnp.int32), pltpu.SMEM((heads,), f32),
             V((tok, ch), bf), V((tok, ch), bf), V((ch, tok), bf), V((ch, tok), bf),
             V((ch, tok), bf), V((ch, tok), bf), V((ch, tok), bf), V((ch, BLOCK), bf),
             V((7, BLOCK, BLOCK), bf), V((ch, tok), f32), V((ch, tok), f32),
@@ -511,14 +522,14 @@
             V((nz, SHARD, width), bf), V((1, 128), f32), V((nx, SHARD, width), bf), V((nx, 1, 128), f32),
             V((nx, SHARD, width), bf), V((levels_out, 2, nz, SHARD, width), bf),
             V((1, tok), f32), V((ny, 1, tok), f32),
-            dma((2,)), dma((2,)), dma((2,)), dma((2,)), dma((2,)), dma((2,)), dma((2,)),
+            dma((10,)), dma((2,)), dma((2,)), dma((2,)), dma((2,)), dma((2,)), dma((2,)),
             dma((levels_out,)), dma((levels_out,)), dma((bx,)), dma((bx,)), dma((levels_out,)), dma((levels_out,)),
             dma, dma,
         ],
-        compiler_params=pltpu.CompilerParams(collective_id=0, has_side_effects=True, vmem_limit_bytes=50 << 20),
+        compiler_params=pltpu.CompilerParams(collective_id=0, has_side_effects=True, vmem_limit_bytes=67043328),
     )(
-        values_in, gate_in, key_proj, query_proj, step_size, log_decay, level_table, level_pick.reshape(1, tok),
-        doc_start, skip_weight,
+        values_in, gate_in, key_proj, query_proj, step_size.T, log_decay.T, level_table.transpose(2, 0, 1),
+        level_pick.reshape(1, tok), doc_start, skip_weight,
     )
     mean_square = squares[0] / (ch * ny)
     return (gated * lax.rsqrt(mean_square + epsilon)[:, None] * norm_gain[None, :]).astype(bf)

time: 73.8 us -> 62.7 us (0.85)
  local copies, waits for them, and re-layouts: 9.08 us -> 0 us
  Pallas kernels: 61.4 us -> 59.4 us
    unnamed x19 -> x0, local copies, waits for them, and re-layouts: 9.08 us -> none
    pallas_call x1, Pallas kernels: 61.4 us -> 59.4 us  [local(): pl.pallas_call(functools.partial(layer_kernel, nx, nz, ny), name='layer',...]
where the time goes in v3:
time: 62.7 us; the launch traced here: 62.6 us
  Pallas kernels  59.4 us (95%)
  other arithmetic  3.19 us (5%)
    pallas_call x1, Pallas kernels, local(): pl.pallas_call(functools.partial(layer_kernel, nx, nz, ny), name='layer',...  59.4 us
    convert_element_type x1, other arithmetic, local(): (gated * lax.rsqrt(mean_square + epsilon)[:, None] * norm_gain[None, :])....  2.51 us

profile of v3, /device:TPU:38, one launch (start us, length us, event | category | flops | bytes accessed | tf_op | source)
XLA Modules:
  0.0 62.6 jit_solution(3455011095265154418)
XLA Ops:
  0.0 59.4 %layer.1 = (bf16[512,1024]{1,0:T(8,128)(2,1)}, f32[1,512]{1,0:T(1,128)}) custom-call(bf16[512,1024]{1,0:T(8,128)(2,1)} %val_hbm.1, bf16[512,1024]{1,0:T(8,128)(2,1)} %gate_hbm.1, bf16[512,128]{1,0:T(8,128)(2,1)} %key_hbm.1, bf16[512,128]{1,0:T(8,128)(2,1)} %query_hbm.1, f32[16,512]{1,0:T(8,128)} %bitcast.6, f32[16,512]{1,0:T(8,128)} %bitcast.7, ...), custom_call_target="tpu_custom_call" | custom-call | tf_op jit(solution)/shard_map/layer/pallas_call | solution.py:507
  59.4 0.7 %add_rsqrt_fusion = f32[1,512]{1,0:T(1,128)S(1)} fusion(f32[1,512]{1,0:T(1,128)} %get-tuple-element.8), kind=kLoop, calls=%fused_computation.1 | loop fusion | flops 1024 | bytes 4096 | tf_op jit(solution)/shard_map/rsqrt | solution.py:535
  60.1 2.5 %multiply_convert_fusion = bf16[512,1024]{1,0:T(8,128)(2,1)} fusion(bf16[512,1024]{1,0:T(8,128)(2,1)} %get-tuple-element.7, f32[1024]{0:T(1024)} %param.18, f32[512]{0:T(512)S(1)} %bitcast.8), kind=kLoop, calls=%fused_computation | loop fusion | flops 2097152 | bytes 2103296 | tf_op jit(solution)/shard_map/convert_element_type | solution.py:535

commit v4 on v3

--- a/solution.py
+++ b/solution.py
@@ -71,6 +71,9 @@
     other = 1 - my_c
     half_heads = heads // 2
 
+    def far_first(i, size):
+        return size // 2 + (i + 1) // 2 * (1 - 2 * lax.rem(i, 2))
+
     def place(z):
         return lax.rem(z, 4) * quads + z // 4
 
@@ -187,13 +190,19 @@
     for s in range(nz):
         merge_pair(s, 0)
 
-    def send_z(o, c):
-        to = lax.rem(my_z + o, nz)
+    def send_z(i, c):
+        to = lax.rem(my_z + far_first(i, nz), nz)
         remote(a_half.at[place(to)], inz.at[my_z], z_s.at[0], z_r.at[0], {"seq_1": to}).start()
         remote(dc, dz.at[my_z], z_s.at[1], z_r.at[1], {"seq_1": to}).start()
         return c
 
-    lax.fori_loop(1, nz, send_z, 0)
+    lax.fori_loop(0, nz - 1, send_z, 0)
+    step_up = remote(a_half, rs.at[0, my_c], lev_s.at[0], lev_r.at[0], {"seq_1": lax.rem(my_z + 1, nz)})
+
+    @pl.when(jnp.logical_not(bit(my_z, 0)))
+    def _():
+        step_up.start()
+
     inz[my_z] = a_half[place(my_z)]
     dz[my_z] = dc[...]
 
@@ -283,19 +292,47 @@
         row_product = row_product * rows_d[z]
     drow[...] = row_product
 
-    def send_x(o, c):
-        to = lax.rem(my_x + o, nx)
+    def send_x(i, c):
+        to = lax.rem(my_x + far_first(i, nx), nx)
         remote(outz.at[total_z], xr.at[my_x], x_s.at[0], x_r.at[0], {"seq_0": to}).start()
         remote(drow, dxr.at[my_x], x_s.at[1], x_r.at[1], {"seq_0": to}).start()
         return c
 
-    lax.fori_loop(1, nx, send_x, 0)
+    lax.fori_loop(0, nx - 1, send_x, 0)
     xr[my_x] = outz[total_z]
     dxr[my_x] = drow[...]
 
+    near = 2
+    quarter = my_z // 4
+
+    def send_levels_quad():
+        for j in range(near, bz):
+            for o in sorted(range(1, quads), key=lambda o: -min(o, quads - o)):
+                to = lax.rem(my_z + 4 * o, nz)
+                @pl.when(bit(to, j))
+                def _():
+                    remote(
+                        outz.at[base_z[j] + to // (1 << (j + 1))], rs.at[j, my_c, place(my_z)],
+                        lev_s.at[j], lev_r.at[j], {"seq_1": to},
+                    ).start()
+
+            @pl.when(bit(my_z, j))
+            def _():
+                rs[j, my_c, place(my_z)] = outz[base_z[j] + my_z // (1 << (j + 1))]
+
+    def pass_levels_quad():
+        for j in range(near, bz):
+            @pl.when(bit(my_z, j))
+            def _():
+                wait_bytes(rs.at[j, 0, pl.ds(0, quads - 1)], lev_r.at[j])
+                for o in range(1, 4):
+                    part = rs.at[j, my_c, pl.ds(lax.rem(my_z, 4) * quads, quads)]
+                    to = quarter * 4 + lax.rem(my_z + o, 4)
+                    remote(part, part, two_s.at[bx + j - near], two_r.at[bx + j - near], {"seq_1": to}).start()
+
     def send_levels_z(wanted):
-        def step(o, c):
-            to = lax.rem(my_z + o, nz)
+        def step(i, c):
+            to = lax.rem(my_z + far_first(i, nz), nz)
             for j in wanted:
                 @pl.when(bit(to, j))
                 def _():
@@ -305,13 +342,13 @@
                     ).start()
             return c
 
-        lax.fori_loop(1, nz, step, 0)
+        lax.fori_loop(0, nz - 1, step, 0)
         for j in wanted:
             @pl.when(bit(my_z, j))
             def _():
                 rs[j, my_c, place(my_z)] = outz[base_z[j] + my_z // (1 << (j + 1))]
 
-    send_levels_z(range(bz // 2, bz))
+    send_levels_quad()
 
     one = jnp.ones_like(d0)
     mine = jnp.where(first, one, d0)
@@ -344,14 +381,14 @@
         @pl.when(bit(my_x, j))
         def _():
             at = base_x[j] + my_x // (1 << (j + 1))
-            for o in range(1, quads):
+            for o in sorted(range(1, quads), key=lambda o: -min(o, quads - o)):
                 to = lax.rem(my_z + 4 * o, nz)
                 remote(
                     outx.at[at], rs.at[bz + j, my_c, place(my_z)], lev_s.at[bz + j], lev_r.at[bz + j], {"seq_1": to}
                 ).start()
             rs[bz + j, my_c, place(my_z)] = outx[at]
 
-    send_levels_z(range(bz // 2))
+    send_levels_z(range(1, near))
     for j in range(bx):
         low = my_x // (1 << j) * (1 << j)
         product = row_lead
@@ -369,13 +406,14 @@
 
     lax.fori_loop(0, heads // 2, gate_pair, 0)
 
+    pass_levels_quad()
     residue = lax.rem(my_z, 4) * quads
     for j in range(bx):
         @pl.when(bit(my_x, j))
         def _():
             if quads > 1:
                 wait_bytes(rs.at[bz + j, 0, pl.ds(0, quads - 1)], lev_r.at[bz + j])
-            for o in (1, nz - 1, 2):
+            for o in (2 if j % 2 == 0 else nz - 2, 1, nz - 1):
                 part = rs.at[bz + j, my_c, pl.ds(residue, quads)]
                 remote(part, part, two_s.at[j], two_r.at[j], {"seq_1": lax.rem(my_z + o, nz)}).start()
 
@@ -409,34 +447,51 @@
             return lambda m: rs[v, m // half_chunks, pl.ds(lax.rem(m, half_chunks) * n, n)].reshape(BLOCK, 128)
         return lambda m: jnp.concatenate([rs[v, 0].reshape(BLOCK // 2, 128), rs[v, 1].reshape(BLOCK // 2, 128)])
 
-    for j in reversed(range(bz)):
+    def arrive_z(j):
         @pl.when(bit(my_z, j))
         def _():
-            wait_bytes(rs.at[j, 0, pl.ds(0, nz - 1)], lev_r.at[j])
+            if j == 0:
+                wait_bytes(rs.at[0, 0], lev_r.at[0])
+            elif j < near:
+                wait_bytes(rs.at[j, 0, pl.ds(0, nz - 1)], lev_r.at[j])
+            else:
+                wait_bytes(rs.at[j, 0, pl.ds(0, 3 * quads)], two_r.at[bx + j - near])
             swap(j).start()
 
-    for j in reversed(range(bz)):
+    def apply_z(j):
         @pl.when(bit(my_z, j))
         def _():
             swap(j).wait()
             apply(low_bits + 2 + j, level_block(j), (0, chunks))
 
+    early = [0] + list(range(near, bz))
+    for j in early:
+        arrive_z(j)
+    for j in early:
+        apply_z(j)
     for j in range(bx):
         @pl.when(bit(my_x, j))
         def _():
             wait_bytes(rs.at[bz + j, 0, pl.ds(0, 3 * quads)], two_r.at[j])
             swap(bz + j).start()
-
+    for j in range(1, near):
+        arrive_z(j)
+    if half_chunks:
+        for j in range(bx):
+            @pl.when(bit(my_x, j))
+            def _():
+                v = bz + j
+                apply(low_bits + 2 + v, level_block(v), (my_c * half_chunks, (my_c + 1) * half_chunks))
+    for j in range(1, near):
+        apply_z(j)
     for j in range(bx):
         @pl.when(bit(my_x, j))
         def _():
             v = bz + j
+            swap(v).wait()
             if half_chunks:
-                apply(low_bits + 2 + v, level_block(v), (my_c * half_chunks, (my_c + 1) * half_chunks))
-                swap(v).wait()
                 apply(low_bits + 2 + v, level_block(v), (other * half_chunks, (other + 1) * half_chunks))
             else:
-                swap(v).wait()
                 apply(low_bits + 2 + v, level_block(v), (0, chunks))
 
     def gate_rows(k, squares):
@@ -465,7 +520,21 @@
     wait_bytes(dz.at[pl.ds(0, nz - 1)], z_s.at[1])
     wait_bytes(xr.at[pl.ds(0, nx - 1)], x_s.at[0])
     wait_bytes(dxr.at[pl.ds(0, nx - 1)], x_s.at[1])
-    for j in range(bz):
+    for j in range(near, bz):
+        reached = (bit(my_z, j)).astype(jnp.int32)
+        for count in range(quads // 2 - 1, quads // 2 + 1):
+            @pl.when((quads // 2 - reached == count) & (count > 0))
+            def _():
+                wait_bytes(inz.at[pl.ds(0, max(count, 1))], lev_s.at[j])
+
+        @pl.when(bit(my_z, j))
+        def _():
+            wait_bytes(rs.at[j, 0, pl.ds(0, 3 * quads)], two_s.at[bx + j - near])
+    @pl.when(jnp.logical_not(bit(my_z, 0)))
+    def _():
+        wait_bytes(a_half, lev_s.at[0])
+
+    for j in range(1, near):
         @pl.when(bit(my_z, j))
         def _():
             if nz // 2 > 1:
@@ -523,7 +592,7 @@
             V((nx, SHARD, width), bf), V((levels_out, 2, nz, SHARD, width), bf),
             V((1, tok), f32), V((ny, 1, tok), f32),
             dma((10,)), dma((2,)), dma((2,)), dma((2,)), dma((2,)), dma((2,)), dma((2,)),
-            dma((levels_out,)), dma((levels_out,)), dma((bx,)), dma((bx,)), dma((levels_out,)), dma((levels_out,)),
+            dma((levels_out,)), dma((levels_out,)), dma((2 * levels_out,)), dma((2 * levels_out,)), dma((levels_out,)), dma((levels_out,)),
             dma, dma,
         ],
         compiler_params=pltpu.CompilerParams(collective_id=0, has_side_effects=True, vmem_limit_bytes=67043328),

time: 62.7 us -> 52.7 us (0.84)
  the two profiles are of different devices: /device:TPU:38 before, /device:TPU:6 now
where the time goes in v4:
time: 52.7 us; the launch traced here: 52.5 us
  Pallas kernels  49.3 us (94%)
  other arithmetic  3.19 us (6%)
    pallas_call x1, Pallas kernels, local(): pl.pallas_call(functools.partial(layer_kernel, nx, nz, ny), name='layer',...  49.3 us
    convert_element_type x1, other arithmetic, local(): (gated * lax.rsqrt(mean_square + epsilon)[:, None] * norm_gain[None, :])....  2.51 us

profile of v4, /device:TPU:6, one launch (start us, length us, event | category | flops | bytes accessed | tf_op | source)
XLA Modules:
  0.0 52.5 jit_solution(2324671875232846501)
XLA Ops:
  0.0 49.3 %layer.1 = (bf16[512,1024]{1,0:T(8,128)(2,1)}, f32[1,512]{1,0:T(1,128)}) custom-call(bf16[512,1024]{1,0:T(8,128)(2,1)} %val_hbm.1, bf16[512,1024]{1,0:T(8,128)(2,1)} %gate_hbm.1, bf16[512,128]{1,0:T(8,128)(2,1)} %key_hbm.1, bf16[512,128]{1,0:T(8,128)(2,1)} %query_hbm.1, f32[16,512]{1,0:T(8,128)} %bitcast.6, f32[16,512]{1,0:T(8,128)} %bitcast.7, ...), custom_call_target="tpu_custom_call" | custom-call | tf_op jit(solution)/shard_map/layer/pallas_call | solution.py:576
  49.3 0.7 %add_rsqrt_fusion = f32[1,512]{1,0:T(1,128)S(1)} fusion(f32[1,512]{1,0:T(1,128)} %get-tuple-element.8), kind=kLoop, calls=%fused_computation.1 | loop fusion | flops 1024 | bytes 4096 | tf_op jit(solution)/shard_map/rsqrt | solution.py:604
  50.0 2.5 %multiply_convert_fusion = bf16[512,1024]{1,0:T(8,128)(2,1)} fusion(bf16[512,1024]{1,0:T(8,128)(2,1)} %get-tuple-element.7, f32[1024]{0:T(1024)} %param.18, f32[512]{0:T(512)S(1)} %bitcast.8), kind=kLoop, calls=%fused_computation | loop fusion | flops 2097152 | bytes 2103296 | tf_op jit(solution)/shard_map/convert_element_type | solution.py:604

commit v5 on v4

--- a/solution.py
+++ b/solution.py
@@ -55,7 +55,7 @@
     key_ref, query_ref, log_ref, table_ref, pick_ref, doc_ref, skip_ref,
     val_v, gate_v, val_t, scaled_t, var0, var1, var2, var3, rhs, acc_t, silu_t, steps, cuts, rows_s, rows_t,
     e_buf, d_buf, pe, pd, a_half, dc, inz, dz, outz, drow, xr, dxr, outx, rs, sq_own, sq,
-    load_s, pair_s, pair_r, z_s, z_r, x_s, x_r, lev_s, lev_r, two_s, two_r, fin_s, fin_r, y_s, y_r,
+    load_s, pair_s, pair_r, z_s, z_r, x_s, x_r, lev_s, lev_r, two_s, two_r, row_r, fin_s, fin_r, y_s, y_r, out_s,
 ):
     f32, bf = jnp.float32, jnp.bfloat16
     tok, ch = val_v.shape
@@ -171,20 +171,20 @@
         rows_t[v] = w
 
     cd.wait()
-    ce.wait()
     first = my_c == 0
     d_own, d_oth = d_buf[...], pd[...]
     d0 = jnp.where(first, d_own, d_oth)
     d1 = jnp.where(first, d_oth, d_own)
     dc[...] = d0 * d1
+    scales = [lane_pick(d1, my_c * half_heads + h) for h in range(half_heads)]
+    ce.wait()
 
     def merge_pair(s, c):
         own = e_buf[my_c * nz + s].astype(f32)
         oth = pe[my_c * nz + s].astype(f32)
         e0 = jnp.where(first, own, oth)
         e1 = jnp.where(first, oth, own)
-        scale = lane_pick(d1, my_c * half_heads + s * SHARD // HEADDIM)
-        a_half[s] = (e1 + scale * e0).astype(bf)
+        a_half[s] = (e1 + scales[s * SHARD // HEADDIM] * e0).astype(bf)
         return c
 
     for s in range(nz):
@@ -276,33 +276,47 @@
     lax.fori_loop(0, ch // BLOCK, inner, 0)
 
     wait_bytes(dz.at[pl.ds(0, nz - 1)], z_r.at[1])
-    wait_bytes(inz.at[pl.ds(0, nz - 1)], z_r.at[0])
     my_head = my_c * half_heads + place(my_z) * SHARD // HEADDIM
     rows_d = [dz[z] for z in range(nz)]
-    state = [inz[z].astype(f32) for z in range(nz)]
-    decay = [lane_pick(r, my_head) for r in rows_d]
+    decay = [[lane_pick(r, my_head) for r in rows_d]]
     for j in range(bz):
-        for m in range(0, nz >> j, 2):
-            outz[base_z[j] + m // 2] = state[m].astype(bf)
-        state = [state[m + 1] + decay[m + 1] * state[m] for m in range(0, nz >> j, 2)]
-        decay = [decay[m + 1] * decay[m] for m in range(0, nz >> j, 2)]
-    outz[total_z] = state[0].astype(bf)
+        decay.append([decay[j][m + 1] * decay[j][m] for m in range(0, nz >> j, 2)])
     row_product = rows_d[0]
     for z in range(1, nz):
         row_product = row_product * rows_d[z]
     drow[...] = row_product
 
+    def send_x_decay(i, c):
+        to = lax.rem(my_x + far_first(i, nx), nx)
+        remote(drow, dxr.at[my_x], x_s.at[1], x_r.at[1], {"seq_0": to}).start()
+        return c
+
+    lax.fori_loop(0, nx - 1, send_x_decay, 0)
+    dxr[my_x] = drow[...]
+    wait_bytes(inz.at[pl.ds(0, nz - 1)], z_r.at[0])
+    state = [[inz[z].astype(f32) for z in range(nz)]]
+    for j in range(bz):
+        state.append([state[j][m + 1] + decay[j][m + 1] * state[j][m] for m in range(0, nz >> j, 2)])
+    outz[total_z] = state[bz][0].astype(bf)
+    for j in range(bz):
+        for m in range(0, nz >> j, 2):
+            outz[base_z[j] + m // 2] = state[j][m].astype(bf)
+
     def send_x(i, c):
         to = lax.rem(my_x + far_first(i, nx), nx)
         remote(outz.at[total_z], xr.at[my_x], x_s.at[0], x_r.at[0], {"seq_0": to}).start()
-        remote(drow, dxr.at[my_x], x_s.at[1], x_r.at[1], {"seq_0": to}).start()
         return c
 
     lax.fori_loop(0, nx - 1, send_x, 0)
     xr[my_x] = outz[total_z]
-    dxr[my_x] = drow[...]
-
     near = 2
+
+    def pass_row(j, o):
+        shard = rs.at[bz + j, my_c, lax.rem(my_z, 4) * quads + lax.rem(my_z // 4 + quads - o, quads)]
+        if o:
+            wait_bytes(shard, row_r.at[j * quads + o])
+        for to in (2 if j % 2 == 0 else nz - 2, 1, nz - 1):
+            remote(shard, shard, two_s.at[j], two_r.at[j], {"seq_1": lax.rem(my_z + to, nz)}).start()
     quarter = my_z // 4
 
     def send_levels_quad():
@@ -368,10 +382,10 @@
         row_lead = row_lead * jnp.where(z < my_z, rows_d[z], one)
 
     wait_bytes(dxr.at[pl.ds(0, nx - 1)], x_r.at[1])
+    rows_x = [dxr[x] for x in range(nx)]
+    decay = [lane_pick(r, my_head) for r in rows_x]
     wait_bytes(xr.at[pl.ds(0, nx - 1)], x_r.at[0])
-    rows_x = [dxr[x] for x in range(nx)]
     state = [xr[x].astype(f32) for x in range(nx)]
-    decay = [lane_pick(r, my_head) for r in rows_x]
     for j in range(bx):
         for m in range(0, nx >> j, 2):
             outx[base_x[j] + m // 2] = state[m].astype(bf)
@@ -384,9 +398,10 @@
             for o in sorted(range(1, quads), key=lambda o: -min(o, quads - o)):
                 to = lax.rem(my_z + 4 * o, nz)
                 remote(
-                    outx.at[at], rs.at[bz + j, my_c, place(my_z)], lev_s.at[bz + j], lev_r.at[bz + j], {"seq_1": to}
+                    outx.at[at], rs.at[bz + j, my_c, place(my_z)], lev_s.at[bz + j], row_r.at[j * quads + o], {"seq_1": to}
                 ).start()
             rs[bz + j, my_c, place(my_z)] = outx[at]
+            pass_row(j, 0)
 
     send_levels_z(range(1, near))
     for j in range(bx):
@@ -407,15 +422,11 @@
     lax.fori_loop(0, heads // 2, gate_pair, 0)
 
     pass_levels_quad()
-    residue = lax.rem(my_z, 4) * quads
-    for j in range(bx):
-        @pl.when(bit(my_x, j))
-        def _():
-            if quads > 1:
-                wait_bytes(rs.at[bz + j, 0, pl.ds(0, quads - 1)], lev_r.at[bz + j])
-            for o in (2 if j % 2 == 0 else nz - 2, 1, nz - 1):
-                part = rs.at[bz + j, my_c, pl.ds(residue, quads)]
-                remote(part, part, two_s.at[j], two_r.at[j], {"seq_1": lax.rem(my_z + o, nz)}).start()
+    for o in sorted(range(1, quads), key=lambda o: min(o, quads - o)):
+        for j in range(bx):
+            @pl.when(bit(my_x, j))
+            def _():
+                pass_row(j, o)
 
     def apply(v, ref, rows):
         def step(m, c):
@@ -509,12 +520,15 @@
     lax.fori_loop(1, ny, send_y, 0)
     sq[my_y] = sq_own[...]
 
-    def back(k, c):
-        at = pl.multiple_of(k * 128, 128)
-        gated_out[:, pl.ds(at, 128)] = acc_t[pl.ds(at, 128), :].T.astype(bf)
-        return c
-
-    lax.fori_loop(0, heads // 2, back, 0)
+    for k in range(heads // 2):
+        part = pl.ds(k * 128, 128)
+        val_v[:, part] = acc_t[part, :].T.astype(bf)
+        if k:
+            part = pl.ds(k * 128 - 128, 128)
+            pltpu.make_async_copy(val_v.at[:, part], gated_out.at[:, part], out_s).start()
+
+    part = pl.ds(ch - 128, 128)
+    pltpu.make_async_copy(val_v.at[:, part], gated_out.at[:, part], out_s).start()
 
     wait_bytes(a_half.at[pl.ds(0, nz - 1)], z_s.at[0])
     wait_bytes(dz.at[pl.ds(0, nz - 1)], z_s.at[1])
@@ -555,7 +569,34 @@
     squares = sq[0]
     for y in range(1, ny):
         squares = squares + sq[y]
+    wait_bytes(val_v, out_s)
     square_out[...] = squares
+
+
+def finish_kernel(count, gated_hbm, square_hbm, gain_hbm, out_hbm, gated, done, squares, gain, small_s, in_s, out_s):
+    tok, ch = gated.shape
+    rows = tok // 8
+    small = [
+        pltpu.make_async_copy(square_hbm, squares, small_s.at[0]), pltpu.make_async_copy(gain_hbm, gain, small_s.at[1]),
+    ]
+    parts = [pl.ds(k * rows, rows) for k in range(8)]
+    loads = [pltpu.make_async_copy(gated_hbm.at[part], gated.at[part], in_s.at[k]) for k, part in enumerate(parts)]
+    stores = [pltpu.make_async_copy(done.at[part], out_hbm.at[part], out_s.at[k]) for k, part in enumerate(parts)]
+    for copy in small + loads:
+        copy.start()
+    for copy in small:
+        copy.wait()
+    scale = lax.rsqrt(squares[...] / count + epsilon)
+    column = jnp.broadcast_to(scale, (128, tok)).T[:, :1]
+    weight = gain[...]
+    for k, part in enumerate(parts):
+        loads[k].wait()
+        done[part, :] = (gated[part, :].astype(jnp.float32) * column[k * rows : (k + 1) * rows] * weight).astype(jnp.bfloat16)
+        if k:
+            stores[k - 1].start()
+    stores[7].start()
+    for copy in stores:
+        copy.wait()
 
 
 def local(
@@ -578,7 +619,7 @@
         name="layer",
         out_shape=(jax.ShapeDtypeStruct((tok, ch), bf), jax.ShapeDtypeStruct((1, tok), f32)),
         in_specs=[hbm] * 10,
-        out_specs=(vmem, vmem),
+        out_specs=(hbm, vmem),
         scratch_shapes=[
             V((tok, width), bf), V((tok, width), bf), V((heads, tok), f32), V((table_levels, level_table.shape[0], heads), f32),
             V((1, tok), jnp.int32), pltpu.SMEM((doc_start.shape[0],), jnp.int32), pltpu.SMEM((heads,), f32),
@@ -592,16 +633,23 @@
             V((nx, SHARD, width), bf), V((levels_out, 2, nz, SHARD, width), bf),
             V((1, tok), f32), V((ny, 1, tok), f32),
             dma((10,)), dma((2,)), dma((2,)), dma((2,)), dma((2,)), dma((2,)), dma((2,)),
-            dma((levels_out,)), dma((levels_out,)), dma((2 * levels_out,)), dma((2 * levels_out,)), dma((levels_out,)), dma((levels_out,)),
-            dma, dma,
+            dma((levels_out,)), dma((levels_out,)), dma((2 * levels_out,)), dma((2 * levels_out,)), dma((bx * nz // 4,)), dma((levels_out,)), dma((levels_out,)),
+            dma, dma, dma,
         ],
         compiler_params=pltpu.CompilerParams(collective_id=0, has_side_effects=True, vmem_limit_bytes=67043328),
     )(
         values_in, gate_in, key_proj, query_proj, step_size.T, log_decay.T, level_table.transpose(2, 0, 1),
         level_pick.reshape(1, tok), doc_start, skip_weight,
     )
-    mean_square = squares[0] / (ch * ny)
-    return (gated * lax.rsqrt(mean_square + epsilon)[:, None] * norm_gain[None, :]).astype(bf)
+    return pl.pallas_call(
+        functools.partial(finish_kernel, ch * ny),
+        name="finish",
+        out_shape=jax.ShapeDtypeStruct((tok, ch), bf),
+        in_specs=[hbm] * 3,
+        out_specs=hbm,
+        scratch_shapes=[V((tok, ch), bf), V((tok, ch), bf), V((1, tok), f32), V((1, ch), f32), dma((2,)), dma((8,)), dma((8,))],
+        compiler_params=pltpu.CompilerParams(vmem_limit_bytes=67043328),
+    )(gated, squares, norm_gain.reshape(1, ch))
 
 
 def solution(mesh):

time: 52.7 us -> 51.7 us (0.981)
  other arithmetic: 3.19 us -> 0 us
  Pallas kernels: 49.3 us -> 51.6 us
    pallas_call x0 -> x1, Pallas kernels: none -> 2.81 us  [local(): pl.pallas_call(functools.partial(finish_kernel, ch * ny), name='finish',...]
    convert_element_type x1 -> x0, other arithmetic: 2.51 us -> none  [local(): (gated * lax.rsqrt(mean_square + epsilon)[:, None] * norm_gain[None, :])....]
    rsqrt x1 -> x0, other arithmetic: 0.69 us -> none  [local(): lax.rsqrt(mean_square + epsilon)[:, None]]
    pallas_call x1, Pallas kernels: 49.3 us -> 48.8 us  [local(): pl.pallas_call(functools.partial(layer_kernel, nx, nz, ny), name='layer',...]
where the time goes in v5:
time: 51.7 us; the launch traced here: 51.6 us
  Pallas kernels  51.6 us (100%)
    pallas_call x1, Pallas kernels, local(): pl.pallas_call(functools.partial(layer_kernel, nx, nz, ny), name='layer',...  48.8 us
    pallas_call x1, Pallas kernels, local(): pl.pallas_call(functools.partial(finish_kernel, ch * ny), name='finish',...  2.81 us

profile of v5, /device:TPU:6, one launch (start us, length us, event | category | flops | bytes accessed | tf_op | source)
XLA Modules:
  0.0 51.6 jit_solution(4455172497380532553)
XLA Ops:
  0.0 48.8 %layer.1 = (bf16[512,1024]{1,0:T(8,128)(2,1)}, f32[1,512]{1,0:T(1,128)}) custom-call(bf16[512,1024]{1,0:T(8,128)(2,1)} %val_hbm.1, bf16[512,1024]{1,0:T(8,128)(2,1)} %gate_hbm.1, bf16[512,128]{1,0:T(8,128)(2,1)} %key_hbm.1, bf16[512,128]{1,0:T(8,128)(2,1)} %query_hbm.1, f32[16,512]{1,0:T(8,128)} %bitcast.6, f32[16,512]{1,0:T(8,128)} %bitcast.7, ...), custom_call_target="tpu_custom_call" | custom-call | tf_op jit(solution)/shard_map/layer/pallas_call | solution.py:617
  48.8 2.8 %finish.1 = bf16[512,1024]{1,0:T(8,128)(2,1)} custom-call(bf16[512,1024]{1,0:T(8,128)(2,1)} %get-tuple-element.7.gated_hbm, f32[1,512]{1,0:T(1,128)} %get-tuple-element.8.square_hbm, f32[1,1024]{1,0:T(1,128)} %bitcast.8), custom_call_target="tpu_custom_call" | custom-call | tf_op jit(solution)/shard_map/finish/pallas_call | solution.py:644

commit v6 on v5

--- a/solution.py
+++ b/solution.py
@@ -391,17 +391,18 @@
             outx[base_x[j] + m // 2] = state[m].astype(bf)
         state = [state[m + 1] + decay[m + 1] * state[m] for m in range(0, nx >> j, 2)]
         decay = [decay[m + 1] * decay[m] for m in range(0, nx >> j, 2)]
-    for j in range(bx):
-        @pl.when(bit(my_x, j))
-        def _():
-            at = base_x[j] + my_x // (1 << (j + 1))
-            for o in sorted(range(1, quads), key=lambda o: -min(o, quads - o)):
-                to = lax.rem(my_z + 4 * o, nz)
-                remote(
-                    outx.at[at], rs.at[bz + j, my_c, place(my_z)], lev_s.at[bz + j], row_r.at[j * quads + o], {"seq_1": to}
-                ).start()
-            rs[bz + j, my_c, place(my_z)] = outx[at]
-            pass_row(j, 0)
+    for o in sorted(range(quads), key=lambda o: -min(o, quads - o)):
+        for j in range(bx):
+            @pl.when(bit(my_x, j))
+            def _():
+                at = base_x[j] + my_x // (1 << (j + 1))
+                mine_at = rs.at[bz + j, my_c, place(my_z)]
+                if o:
+                    to = lax.rem(my_z + 4 * o, nz)
+                    remote(outx.at[at], mine_at, lev_s.at[bz + j], row_r.at[j * quads + o], {"seq_1": to}).start()
+                else:
+                    rs[bz + j, my_c, place(my_z)] = outx[at]
+                    pass_row(j, 0)
 
     send_levels_z(range(1, near))
     for j in range(bx):

time: 51.7 us -> 50.9 us (0.985)
  Pallas kernels: 51.6 us -> 50.8 us
    pallas_call x1, Pallas kernels: 48.8 us -> 48 us  [local(): pl.pallas_call(functools.partial(layer_kernel, nx, nz, ny), name='layer',...]
where the time goes in v6:
time: 50.9 us; the launch traced here: 50.8 us
  Pallas kernels  50.8 us (100%)
    pallas_call x1, Pallas kernels, local(): pl.pallas_call(functools.partial(layer_kernel, nx, nz, ny), name='layer',...  48 us
    pallas_call x1, Pallas kernels, local(): pl.pallas_call(functools.partial(finish_kernel, ch * ny), name='finish',...  2.81 us

profile of v6, /device:TPU:6, one launch (start us, length us, event | category | flops | bytes accessed | tf_op | source)
XLA Modules:
  0.0 50.8 jit_solution(7987938279756307381)
XLA Ops:
  0.0 48.0 %layer.1 = (bf16[512,1024]{1,0:T(8,128)(2,1)}, f32[1,512]{1,0:T(1,128)}) custom-call(bf16[512,1024]{1,0:T(8,128)(2,1)} %val_hbm.1, bf16[512,1024]{1,0:T(8,128)(2,1)} %gate_hbm.1, bf16[512,128]{1,0:T(8,128)(2,1)} %key_hbm.1, bf16[512,128]{1,0:T(8,128)(2,1)} %query_hbm.1, f32[16,512]{1,0:T(8,128)} %bitcast.6, f32[16,512]{1,0:T(8,128)} %bitcast.7, ...), custom_call_target="tpu_custom_call" | custom-call | tf_op jit(solution)/shard_map/layer/pallas_call | solution.py:618
  48.0 2.8 %finish.1 = bf16[512,1024]{1,0:T(8,128)(2,1)} custom-call(bf16[512,1024]{1,0:T(8,128)(2,1)} %get-tuple-element.7.gated_hbm, f32[1,512]{1,0:T(1,128)} %get-tuple-element.8.square_hbm, f32[1,1024]{1,0:T(1,128)} %bitcast.8), custom_call_target="tpu_custom_call" | custom-call | tf_op jit(solution)/shard_map/finish/pallas_call | solution.py:645

commit v7 on v6

--- a/solution.py
+++ b/solution.py
@@ -71,20 +71,21 @@
     other = 1 - my_c
     half_heads = heads // 2
 
+    def place(z):
+        return lax.rem(z, 4) * quads + z // 4
+
     def far_first(i, size):
         return size // 2 + (i + 1) // 2 * (1 - 2 * lax.rem(i, 2))
 
-    def place(z):
-        return lax.rem(z, 4) * quads + z // 4
-
     barrier = pltpu.get_barrier_semaphore()
 
     def greet(axis, mine, size):
-        def step(o, c):
-            pl.semaphore_signal(barrier, inc=1, device_id={axis: lax.rem(mine + o, size)}, device_id_type=MESH_ID)
+        def step(i, c):
+            to = lax.rem(mine + far_first(i, size), size)
+            pl.semaphore_signal(barrier, inc=1, device_id={axis: to}, device_id_type=MESH_ID)
             return c
 
-        lax.fori_loop(1, size, step, 0)
+        lax.fori_loop(0, size - 1, step, 0)
 
     greet("seq_1", my_z, nz)
     greet("seq_0", my_x, nx)
@@ -320,8 +321,8 @@
     quarter = my_z // 4
 
     def send_levels_quad():
-        for j in range(near, bz):
-            for o in sorted(range(1, quads), key=lambda o: -min(o, quads - o)):
+        for o in sorted(range(1, quads), key=lambda o: -min(o, quads - o)):
+            for j in range(near, bz):
                 to = lax.rem(my_z + 4 * o, nz)
                 @pl.when(bit(to, j))
                 def _():
@@ -330,6 +331,7 @@
                         lev_s.at[j], lev_r.at[j], {"seq_1": to},
                     ).start()
 
+        for j in range(near, bz):
             @pl.when(bit(my_z, j))
             def _():
                 rs[j, my_c, place(my_z)] = outz[base_z[j] + my_z // (1 << (j + 1))]
@@ -514,11 +516,11 @@
 
     sq_own[...] = lax.fori_loop(0, heads // 2, gate_rows, jnp.zeros((1, tok), f32))
 
-    def send_y(o, c):
-        remote(sq_own, sq.at[my_y], y_s, y_r, {"head": lax.rem(my_y + o, ny)}).start()
-        return c
-
-    lax.fori_loop(1, ny, send_y, 0)
+    def send_y(i, c):
+        remote(sq_own, sq.at[my_y], y_s, y_r, {"head": lax.rem(my_y + far_first(i, ny), ny)}).start()
+        return c
+
+    lax.fori_loop(0, ny - 1, send_y, 0)
     sq[my_y] = sq_own[...]
 
     for k in range(heads // 2):

time: 50.9 us -> 51.5 us (1.012)
    pallas_call x1, Pallas kernels: 48 us -> 48.5 us  [local(): pl.pallas_call(functools.partial(layer_kernel, nx, nz, ny), name='layer',...]
where the time goes in v7:
time: 51.5 us; the launch traced here: 51.3 us
  Pallas kernels  51.3 us (100%)
    pallas_call x1, Pallas kernels, local(): pl.pallas_call(functools.partial(layer_kernel, nx, nz, ny), name='layer',...  48.5 us
    pallas_call x1, Pallas kernels, local(): pl.pallas_call(functools.partial(finish_kernel, ch * ny), name='finish',...  2.81 us

profile of v7, /device:TPU:6, one launch (start us, length us, event | category | flops | bytes accessed | tf_op | source)
XLA Modules:
  0.0 51.3 jit_solution(14620380220427191290)
XLA Ops:
  0.0 48.5 %layer.1 = (bf16[512,1024]{1,0:T(8,128)(2,1)}, f32[1,512]{1,0:T(1,128)}) custom-call(bf16[512,1024]{1,0:T(8,128)(2,1)} %val_hbm.1, bf16[512,1024]{1,0:T(8,128)(2,1)} %gate_hbm.1, bf16[512,128]{1,0:T(8,128)(2,1)} %key_hbm.1, bf16[512,128]{1,0:T(8,128)(2,1)} %query_hbm.1, f32[16,512]{1,0:T(8,128)} %bitcast.6, f32[16,512]{1,0:T(8,128)} %bitcast.7, ...), custom_call_target="tpu_custom_call" | custom-call | tf_op jit(solution)/shard_map/layer/pallas_call | solution.py:620
  48.5 2.8 %finish.1 = bf16[512,1024]{1,0:T(8,128)(2,1)} custom-call(bf16[512,1024]{1,0:T(8,128)(2,1)} %get-tuple-element.7.gated_hbm, f32[1,512]{1,0:T(1,128)} %get-tuple-element.8.square_hbm, f32[1,1024]{1,0:T(1,128)} %bitcast.8), custom_call_target="tpu_custom_call" | custom-call | tf_op jit(solution)/shard_map/finish/pallas_call | solution.py:647
